TPU v7x, 32 devices: a whole 2x2x4 slice. The times are simulated.
32 devices in a mesh: gx: 4 (over y, x), gy: 4 (over z), gz: 2 (over core).
Axes of the slice: x: 2, y: 2, z: 4, core: 2. Of those that a mesh axis runs over, the one named last changes fastest.
Arguments:
- a_blocks: float32 [1664, 7, 128, 128], P(('gx', 'gy', 'gz')), as said below
- block_cols: int32 [1664, 7], P(('gx', 'gy', 'gz')), may hold values from 0 to 363, as said below
- agg_ids: int32 [1664], P(('gx', 'gy', 'gz')), may hold values from 0 to 51, as said below
- agg_counts: int32 [32], P(('gx', 'gy', 'gz')), may hold values from 1 to 52, as said below
- p0_blocks: float32 [1664, 6, 128], P(('gx', 'gy', 'gz')), may hold values from -6 to 6
- start_vec: float32 [1664, 128], P(('gx', 'gy', 'gz'))
Outputs:
- p_blocks: float32 [1664, 7, 6, 128], P(('gx', 'gy', 'gz'))
- p_cols: int32 [1664, 7], P(('gx', 'gy', 'gz'))
- power_vec: float32 [1664, 128], P(('gx', 'gy', 'gz'))
Inputs may be any that keep to these rules, and one draw needn't show every extreme that they name: `block_cols`: entry 0 of each block row names the row itself; every neighbour that an entry names exists. `agg_ids`: below the count of the row's own subdomain. `agg_counts`: some subdomain has 52 aggregates. `a_blocks`: block 0 of each block row has a positive diagonal.
All inputs are finite; a program needn't handle non-finite values.
Results may differ from a plain program's by a relative error of at most 0.0003.
Values sent between devices are 32-bit elements; how exact they have to be, the bound alone decides.
No kernel may reach another device: no remote copies, remote signals or barrier semaphores. Data moves between devices by JAX's collectives and lax.ppermute only.
A program may use at most 128 MiB of HBM per device.

v0:
```python
import jax
import jax.numpy as jnp
from jax import lax
from jax.sharding import PartitionSpec as P

ITERS = 8


precise_mode = lax.Precision.HIGHEST


def carried_in(value, axis, join, neutral):
    count, mine = (lax.axis_size(axis), lax.axis_index(axis))
    pieces = lax.all_gather(value, axis)
    so_far = jnp.full_like(value, 0) + jnp.asarray(neutral, value.dtype)

    def lap(position, so_far):
        longer = join(so_far, pieces[position])
        return jnp.where(position < mine, longer, so_far)

    return lax.fori_loop(0, count - 1, lap, so_far)


def with_halo(cells, sides, width):
    for axis, dim in sides:
        count = lax.axis_size(axis)
        ends = count - 1
        head = lax.slice_in_dim(cells, 0, width, axis=dim)
        tail = lax.slice_in_dim(cells, cells.shape[dim] - width, cells.shape[dim], axis=dim)
        cells = jnp.concatenate(
            [
                lax.ppermute(tail, axis, [(i, (i + 1) % count) for i in range(ends)]),
                cells,
                lax.ppermute(head, axis, [((i + 1) % count, i) for i in range(ends)]),
            ],
            axis=dim,
        )
    return cells


def faces_of(wide):
    return jnp.concatenate(
        [
            wide[1, 1, 1],
            wide[0, 1, 1],
            wide[2, 1, 1],
            wide[1, 0, 1],
            wide[1, 2, 1],
            wide[1, 1, 0],
            wide[1, 1, 2],
        ],
        axis=0,
    )


def add_counts(earlier, later):
    return earlier + later


def offset_of(agg_counts):
    empty = jnp.zeros((1,), jnp.int32)
    return carried_in(agg_counts, ("gx", "gy", "gz"), add_counts, empty)[0]


def local(a_blocks, block_cols, agg_ids, agg_counts, p0_blocks, start_vec):
    diag_values = jnp.diagonal(a_blocks[:, 0], axis1=1, axis2=2)
    entry_total = (
        lax.axis_size("gx")
        * lax.axis_size("gy")
        * lax.axis_size("gz")
        * start_vec.shape[0]
        * start_vec.shape[1]
    )
    root_total = jnp.sqrt(jnp.float32(entry_total))
    previous = start_vec
    current = start_vec
    for turn_index in range(ITERS):
        previous = current
        operate_wide = with_halo(current[None, None, None], (("gx", 0), ("gy", 1), ("gz", 2)), 1)
        picked = faces_of(operate_wide)[block_cols]
        mixed = jnp.einsum("bkij,bkj->bi", a_blocks, picked, precision=precise_mode)
        current = mixed / diag_values
    totals = lax.psum(
        (jnp.sum(previous * previous), jnp.sum(current * current)), ("gx", "gy", "gz")
    )
    last_norm = jnp.sqrt(totals[1])
    spectral = last_norm / jnp.sqrt(totals[0])
    power_vec = current * (root_total / last_norm)
    damping = 4.0 / (3.0 * spectral)
    wide = with_halo(p0_blocks[None, None, None], (("gx", 0), ("gy", 1), ("gz", 2)), 1)
    picked_p0 = faces_of(wide)[block_cols]
    product = jnp.einsum("bksj,bkij->bksi", picked_p0, a_blocks, precision=precise_mode)
    smoothed = -(damping / diag_values)[:, None, None, :] * product
    p_blocks = smoothed.at[:, 0].add(p0_blocks)
    offset = offset_of(agg_counts)
    own_columns = (p0_blocks.shape[1] * (offset + agg_ids)).astype(jnp.int32)
    wide_columns = with_halo(own_columns[None, None, None], (("gx", 0), ("gy", 1), ("gz", 2)), 1)
    p_cols = faces_of(wide_columns)[block_cols]
    return (p_blocks, p_cols, power_vec.astype(jnp.float32))


def solution(mesh):
    in_specs = (
        P(("gx", "gy", "gz"), None, None, None),
        P(("gx", "gy", "gz"), None),
        P(("gx", "gy", "gz")),
        P(("gx", "gy", "gz")),
        P(("gx", "gy", "gz"), None, None),
        P(("gx", "gy", "gz"), None),
    )
    out_specs = (
        P(("gx", "gy", "gz"), None, None, None),
        P(("gx", "gy", "gz"), None),
        P(("gx", "gy", "gz"), None),
    )
    return jax.shard_map(local, mesh=mesh, in_specs=in_specs, out_specs=out_specs, check_vma=False)
```

profile of v0, /device:TPU:0, one launch (start us, length us, event | category | flops | bytes accessed | tf_op | source)
XLA Modules:
  0.0 620.6 jit_solution(1844591081584998334)
XLA Ops:
  0.6 4.9 collective-permute-start
  8.5 5.2 collective-permute-start.48
  15.8 42.3 %all-reduce = s32[32]{0:T(128)S(1)} all-reduce(s32[32]{0:T(128)S(1)} %dynamic-update-slice.3), channel_id=2, replica_groups=mesh['gx'=4,'gy'=4,'gz'=2] {'gx','gy','gz'}, use_global_device_ids=true, to_apply=%add | all-reduce | flops 32 | bytes 256
  58.2 39.5 %while.14 = (s32[]{:T(128)}, s32[1]{0:T(128)}, s32[]{:T(128)}, s32[32,1]{0,1:T(1,128)S(1)}, s32[]{:T(128)}) while((s32[]{:T(128)}, s32[1]{0:T(128)}, s32[]{:T(128)}, s32[32,1]{0,1:T(1,128)S(1)}, s32[]{:T(128)}) %tuple.47), condition=%wide.region_5.6_spmd, body=%wide.region_4.5_spmd.sunk | while | flops 5 | bytes 107 | solution.py:21
  98.4 4.2 collective-permute-start.54
  106.1 4.8 copy.266
  117.7 4.3 collective-permute-done.3
  123.3 3.1 collective-permute-start.4
  129.5 24.7 %fusion.7 = f32[52,1,128,1]{2,1,3,0:T(1,128)S(1)} fusion(f32[52,7,128,1]{2,3,1,0:T(1,128)S(1)} %reshape.179, f32[52,7,128,128]{3,2,1,0:T(8,128)} %param.10), kind=kOutput, calls=%fused_computation.115 | convolution fusion | flops 71565312 | bytes 24068096 | tf_op jit(solution)/shard_map/bkij,bkj->bi/dot_general | solution.py:81
  154.3 4.5 collective-permute-start.6
  160.2 3.3 collective-permute-start.56
  165.0 4.4 collective-permute-start.8
  172.2 5.6 collective-permute-done.9
  179.2 3.5 collective-permute-start.10
  185.2 24.7 %fusion.8 = f32[52,1,128,1]{2,1,3,0:T(1,128)S(1)} fusion(f32[52,7,128,1]{2,3,1,0:T(1,128)S(1)} %reshape.181, f32[52,7,128,128]{3,2,1,0:T(8,128)} %param.10), kind=kOutput, calls=%fused_computation.116 | convolution fusion | flops 71565312 | bytes 24068096 | tf_op jit(solution)/shard_map/bkij,bkj->bi/dot_general | solution.py:81
  209.9 4.9 collective-permute-start.12
  216.4 5.1 collective-permute-done.13
  226.2 4.1 collective-permute-done.15
  231.7 3.1 collective-permute-start.16
  238.0 24.7 %fusion.9 = f32[52,1,128,1]{2,1,3,0:T(1,128)S(1)} fusion(f32[52,7,128,1]{2,3,1,0:T(1,128)S(1)} %reshape.183, f32[52,7,128,128]{3,2,1,0:T(8,128)} %param.10), kind=kOutput, calls=%fused_computation.117 | convolution fusion | flops 71565312 | bytes 24068096 | tf_op jit(solution)/shard_map/bkij,bkj->bi/dot_general | solution.py:81
  262.7 4.8 collective-permute-start.18
  269.1 4.2 collective-permute-done.19
  275.4 2.8 gather_fusion.10
  280.6 4.7 collective-permute-done.21
  286.7 3.1 collective-permute-start.22
  292.7 24.7 %fusion.10 = f32[52,1,128,1]{2,1,3,0:T(1,128)S(1)} fusion(f32[52,7,128,1]{2,3,1,0:T(1,128)S(1)} %reshape.185, f32[52,7,128,128]{3,2,1,0:T(8,128)} %param.10), kind=kOutput, calls=%fused_computation.118 | convolution fusion | flops 71565312 | bytes 24068096 | tf_op jit(solution)/shard_map/bkij,bkj->bi/dot_general | solution.py:81
  317.5 3.0 collective-permute-start.24
  328.2 4.6 collective-permute-start.26
  335.0 3.6 collective-permute-done.26
  338.8 4.7 collective-permute-done.27
  344.9 3.1 collective-permute-start.28
  350.9 24.7 %fusion.11 = f32[52,1,128,1]{2,1,3,0:T(1,128)S(1)} fusion(f32[52,7,128,1]{2,3,1,0:T(1,128)S(1)} %reshape.187, f32[52,7,128,128]{3,2,1,0:T(8,128)} %param.10), kind=kOutput, calls=%fused_computation.119 | convolution fusion | flops 71565312 | bytes 24068096 | tf_op jit(solution)/shard_map/bkij,bkj->bi/dot_general | solution.py:81
  375.6 4.3 collective-permute-start.30
  396.3 4.9 collective-permute-done.33
  402.5 3.3 collective-permute-start.34
  408.5 24.7 %fusion.12 = f32[52,1,128,1]{2,1,3,0:T(1,128)S(1)} fusion(f32[52,7,128,1]{2,3,1,0:T(1,128)S(1)} %reshape.189, f32[52,7,128,128]{3,2,1,0:T(8,128)} %param.10), kind=kOutput, calls=%fused_computation.120 | convolution fusion | flops 71565312 | bytes 24068096 | tf_op jit(solution)/shard_map/bkij,bkj->bi/dot_general | solution.py:81
  433.3 4.0 collective-permute-start.36
  438.8 4.2 collective-permute-done.37
  447.5 4.9 collective-permute-done.39
  453.7 3.1 collective-permute-start.40
  459.7 24.7 %fusion.13 = f32[52,1,128,1]{2,1,3,0:T(1,128)S(1)} fusion(f32[52,7,128,1]{2,3,1,0:T(1,128)S(1)} %reshape.191, f32[52,7,128,128]{3,2,1,0:T(8,128)} %param.10), kind=kOutput, calls=%fused_computation.121 | convolution fusion | flops 71565312 | bytes 24068096 | tf_op jit(solution)/shard_map/bkij,bkj->bi/dot_general | solution.py:81
  485.0 4.6 collective-permute-start.42
  491.9 3.5 collective-permute-done.43
  501.3 4.9 collective-permute-done.45
  507.6 3.1 collective-permute-start.46
  513.5 24.7 %fusion.14 = f32[52,1,128,1]{2,1,3,0:T(1,128)S(1)} fusion(f32[52,7,128,1]{2,3,1,0:T(1,128)S(1)} %reshape.193, f32[52,7,128,128]{3,2,1,0:T(8,128)} %param.10), kind=kOutput, calls=%fused_computation.122 | convolution fusion | flops 71565312 | bytes 24068096 | tf_op jit(solution)/shard_map/bkij,bkj->bi/dot_general | solution.py:81
  538.9 38.1 %all-reduce.1 = (f32[]{:T(128)}, f32[]{:T(128)}) all-reduce(f32[]{:T(128)} %multiply_reduce_fusion.1, f32[]{:T(128)} %get-tuple-element.120), channel_id=1, replica_groups=mesh['gx'=4,'gy'=4,'gz'=2] {'gx','gy','gz'}, use_global_device_ids=true, to_apply=%region_1.2 | all-reduce | flops 2 | bytes 16 | tf_op jit(solution)/shard_map/psum | solution.py:83
  579.0 40.1 %convolution_multiply_fusion = f32[52,7,6,128]{3,2,1,0:T(8,128)S(1)} fusion(f32[52,7,6,128]{3,2,1,0:T(8,128)S(1)} %bitcast.210, f32[52,7,128,128]{3,2,1,0:T(8,128)} %param.10, f32[52,128]{1,0:T(8,128)S(1)} %get-tuple-element.125), kind=kOutput, calls=%fused_computation.13 | convolution fusion | flops 429671424 | bytes 26118144 | tf_op jit(solution)/shard_map/bksj,bkij->bksi/dot_general | solution.py:92
  (272 shorter events, 129.3 us)
Async XLA Ops:
  0.6 112.2 %collective-permute-start = (f32[1,1,1,52,128]{4,3,2,1,0:T(8,128)}, f32[1,1,1,52,128]{4,3,2,1,0:T(8,128)S(1)}, u32[]{:S(2)}, u32[]{:S(2)}) collective-permute-start(f32[1,1,1,52,128]{4,3,2,1,0:T(8,128)} %bitcast.212), channel_id=1, source_target_pairs={{0,8},{8,16},{16,24},{1,9},{9,17},{17,25},{2,10},{10,18},{18,26},{... | collective-permute-start | bytes 79880 | tf_op jit(solution)/shard_map/ppermute | solution.py:32
  5.5 107.3 %collective-permute-start.1 = (f32[1,1,1,52,128]{4,3,2,1,0:T(8,128)}, f32[1,1,1,52,128]{4,3,2,1,0:T(8,128)S(1)}, u32[]{:S(2)}, u32[]{:S(2)}) collective-permute-start(f32[1,1,1,52,128]{4,3,2,1,0:T(8,128)} %bitcast.213), channel_id=1, source_target_pairs={{8,0},{16,8},{24,16},{9,1},{17,9},{25,17},{10,2},{18,10},{26,18},{... | collective-permute-start | bytes 79880 | tf_op jit(solution)/shard_map/ppermute | solution.py:34
  8.5 313.2 %collective-permute-start.48 = (f32[1,1,1,52,6,128]{5,4,3,2,1,0:T(8,128)}, f32[1,1,1,52,6,128]{5,4,3,2,1,0:T(8,128)}, u32[]{:S(2)}, u32[]{:S(2)}) collective-permute-start(f32[1,1,1,52,6,128]{5,4,3,2,1,0:T(8,128)} %get-tuple-element.122), channel_id=1, source_target_pairs={{0,8},{8,16},{16,24},{1,9},{9,17},{17,25},{2,10},{10,18},{18,26},{... | collective-permute-start | bytes 479240 | tf_op jit(solution)/shard_map/ppermute | solution.py:32
  13.8 307.9 %collective-permute-start.49 = (f32[1,1,1,52,6,128]{5,4,3,2,1,0:T(8,128)}, f32[1,1,1,52,6,128]{5,4,3,2,1,0:T(8,128)}, u32[]{:S(2)}, u32[]{:S(2)}) collective-permute-start(f32[1,1,1,52,6,128]{5,4,3,2,1,0:T(8,128)} %get-tuple-element.122), channel_id=1, source_target_pairs={{8,0},{16,8},{24,16},{9,1},{17,9},{25,17},{10,2},{18,10},{26,18},{... | collective-permute-start | bytes 479240 | tf_op jit(solution)/shard_map/ppermute | solution.py:34
  98.4 60.4 %collective-permute-start.54 = (s32[1,1,1,52]{3,2,1,0:T(1,128)S(1)}, s32[1,1,1,52]{3,2,1,0:T(1,128)S(1)}, u32[]{:S(2)}, u32[]{:S(2)}) collective-permute-start(s32[1,1,1,52]{3,2,1,0:T(1,128)S(1)} %fusion.33), channel_id=1, source_target_pairs={{0,8},{8,16},{16,24},{1,9},{9,17},{17,25},{2,10},{10,18},{18,26},{... | collective-permute-start | bytes 632 | tf_op jit(solution)/shard_map/ppermute | solution.py:32
  112.9 4.8 collective-permute-start.2
  115.6 6.4 %collective-permute-start.3 = (f32[3,1,1,52,128]{4,3,2,1,0:T(8,128)S(1)}, f32[3,1,1,52,128]{4,3,2,1,0:T(8,128)S(1)}, u32[]{:S(2)}, u32[]{:S(2)}) collective-permute-start(f32[3,1,1,52,128]{4,3,2,1,0:T(8,128)S(1)} %pad_maximum_fusion.3), channel_id=1, source_target_pairs={{2,0},{4,2},{6,4},{3,1},{5,3},{7,5},{10,8},{12,10},{14,12},{11,9},... | collective-permute-start | bytes 239624 | tf_op jit(solution)/shard_map/ppermute | solution.py:34
  122.0 4.4 collective-permute-start.5
  123.3 4.4 collective-permute-start.4
  126.4 33.8 %collective-permute-start.55 = (s32[1,1,1,52]{3,2,1,0:T(1,128)S(1)}, s32[1,1,1,52]{3,2,1,0:T(1,128)S(1)}, u32[]{:S(2)}, u32[]{:S(2)}) collective-permute-start(s32[1,1,1,52]{3,2,1,0:T(1,128)S(1)} %fusion.33), channel_id=1, source_target_pairs={{8,0},{16,8},{24,16},{9,1},{17,9},{25,17},{10,2},{18,10},{26,18},{... | collective-permute-start | bytes 632 | tf_op jit(solution)/shard_map/ppermute | solution.py:34
  154.3 9.2 %collective-permute-start.6 = (f32[1,1,1,52,128]{4,3,2,1,0:T(8,128)S(1)}, f32[1,1,1,52,128]{4,3,2,1,0:T(8,128)S(1)}, u32[]{:S(2)}, u32[]{:S(2)}) collective-permute-start(f32[1,1,1,52,128]{4,3,2,1,0:T(8,128)S(1)} %bitcast.218), channel_id=1, source_target_pairs={{0,8},{8,16},{16,24},{1,9},{9,17},{17,25},{2,10},{10,18},{18,26},{... | collective-permute-start | bytes 79880 | tf_op jit(solution)/shard_map/ppermute | solution.py:32
  158.8 6.1 collective-permute-start.7
  160.2 9.2 %collective-permute-start.56 = (s32[3,1,1,52]{3,2,1,0:T(1,128)S(1)}, s32[3,1,1,52]{3,2,1,0:T(1,128)S(1)}, u32[]{:S(2)}, u32[]{:S(2)}) collective-permute-start(s32[3,1,1,52]{3,2,1,0:T(1,128)S(1)} %pad_add_fusion.1), channel_id=1, source_target_pairs={{0,2},{2,4},{4,6},{1,3},{3,5},{5,7},{8,10},{10,12},{12,14},{9,11},... | collective-permute-start | bytes 1880 | tf_op jit(solution)/shard_map/ppermute | solution.py:32
  163.5 5.9 collective-permute-start.57
  165.0 7.0 %collective-permute-start.8 = (f32[3,1,1,52,128]{4,3,2,1,0:T(8,128)S(1)}, f32[3,1,1,52,128]{4,3,2,1,0:T(8,128)S(1)}, u32[]{:S(2)}, u32[]{:S(2)}) collective-permute-start(f32[3,1,1,52,128]{4,3,2,1,0:T(8,128)S(1)} %pad_maximum_fusion.4), channel_id=1, source_target_pairs={{0,2},{2,4},{4,6},{1,3},{3,5},{5,7},{8,10},{10,12},{12,14},{9,11},... | collective-permute-start | bytes 239624 | tf_op jit(solution)/shard_map/ppermute | solution.py:32
  169.4 98.2 %collective-permute-start.59 = (s32[3,3,1,52]{3,2,1,0:T(1,128)S(1)}, s32[3,3,1,52]{3,2,1,0:T(1,128)S(1)}, u32[]{:S(2)}, u32[]{:S(2)}) collective-permute-start(s32[3,3,1,52]{3,2,1,0:T(1,128)S(1)} %pad_add_fusion), channel_id=1, source_target_pairs={{1,0},{3,2},{5,4},{7,6},{9,8},{11,10},{13,12},{15,14},{17,16},{19,... | collective-permute-start | bytes 5624 | tf_op jit(solution)/shard_map/ppermute | solution.py:34
  170.7 7.1 %collective-permute-start.9 = (f32[3,1,1,52,128]{4,3,2,1,0:T(8,128)S(1)}, f32[3,1,1,52,128]{4,3,2,1,0:T(8,128)S(1)}, u32[]{:S(2)}, u32[]{:S(2)}) collective-permute-start(f32[3,1,1,52,128]{4,3,2,1,0:T(8,128)S(1)} %pad_maximum_fusion.4), channel_id=1, source_target_pairs={{2,0},{4,2},{6,4},{3,1},{5,3},{7,5},{10,8},{12,10},{14,12},{11,9},... | collective-permute-start | bytes 239624 | tf_op jit(solution)/shard_map/ppermute | solution.py:34
  177.9 4.9 collective-permute-start.11
  209.9 6.4 %collective-permute-start.12 = (f32[1,1,1,52,128]{4,3,2,1,0:T(8,128)S(1)}, f32[1,1,1,52,128]{4,3,2,1,0:T(8,128)S(1)}, u32[]{:S(2)}, u32[]{:S(2)}) collective-permute-start(f32[1,1,1,52,128]{4,3,2,1,0:T(8,128)S(1)} %bitcast.236), channel_id=1, source_target_pairs={{0,8},{8,16},{16,24},{1,9},{9,17},{17,25},{2,10},{10,18},{18,26},{... | collective-permute-start | bytes 79880 | tf_op jit(solution)/shard_map/ppermute | solution.py:32
  214.8 6.7 %collective-permute-start.13 = (f32[1,1,1,52,128]{4,3,2,1,0:T(8,128)S(1)}, f32[1,1,1,52,128]{4,3,2,1,0:T(8,128)S(1)}, u32[]{:S(2)}, u32[]{:S(2)}) collective-permute-start(f32[1,1,1,52,128]{4,3,2,1,0:T(8,128)S(1)} %bitcast.237), channel_id=1, source_target_pairs={{8,0},{16,8},{24,16},{9,1},{17,9},{25,17},{10,2},{18,10},{26,18},{... | collective-permute-start | bytes 79880 | tf_op jit(solution)/shard_map/ppermute | solution.py:34
  221.5 4.5 collective-permute-start.14
  224.0 6.4 %collective-permute-start.15 = (f32[3,1,1,52,128]{4,3,2,1,0:T(8,128)S(1)}, f32[3,1,1,52,128]{4,3,2,1,0:T(8,128)S(1)}, u32[]{:S(2)}, u32[]{:S(2)}) collective-permute-start(f32[3,1,1,52,128]{4,3,2,1,0:T(8,128)S(1)} %pad_maximum_fusion.5), channel_id=1, source_target_pairs={{2,0},{4,2},{6,4},{3,1},{5,3},{7,5},{10,8},{12,10},{14,12},{11,9},... | collective-permute-start | bytes 239624 | tf_op jit(solution)/shard_map/ppermute | solution.py:34
  231.7 4.4 collective-permute-start.16
  234.8 40.4 %collective-permute-start.58 = (s32[3,3,1,52]{3,2,1,0:T(1,128)S(1)}, s32[3,3,1,52]{3,2,1,0:T(1,128)S(1)}, u32[]{:S(2)}, u32[]{:S(2)}) collective-permute-start(s32[3,3,1,52]{3,2,1,0:T(1,128)S(1)} %pad_add_fusion), channel_id=1, source_target_pairs={{0,1},{2,3},{4,5},{6,7},{8,9},{10,11},{12,13},{14,15},{16,17},{18,... | collective-permute-start | bytes 5624 | tf_op jit(solution)/shard_map/ppermute | solution.py:32
  262.7 6.4 %collective-permute-start.18 = (f32[1,1,1,52,128]{4,3,2,1,0:T(8,128)S(1)}, f32[1,1,1,52,128]{4,3,2,1,0:T(8,128)S(1)}, u32[]{:S(2)}, u32[]{:S(2)}) collective-permute-start(f32[1,1,1,52,128]{4,3,2,1,0:T(8,128)S(1)} %bitcast.224), channel_id=1, source_target_pairs={{0,8},{8,16},{16,24},{1,9},{9,17},{17,25},{2,10},{10,18},{18,26},{... | collective-permute-start | bytes 79880 | tf_op jit(solution)/shard_map/ppermute | solution.py:32
  267.6 5.8 collective-permute-start.19
  273.3 7.1 %collective-permute-start.20 = (f32[3,1,1,52,128]{4,3,2,1,0:T(8,128)S(1)}, f32[3,1,1,52,128]{4,3,2,1,0:T(8,128)S(1)}, u32[]{:S(2)}, u32[]{:S(2)}) collective-permute-start(f32[3,1,1,52,128]{4,3,2,1,0:T(8,128)S(1)} %pad_maximum_fusion.6), channel_id=1, source_target_pairs={{0,2},{2,4},{4,6},{1,3},{3,5},{5,7},{8,10},{10,12},{12,14},{9,11},... | collective-permute-start | bytes 239624 | tf_op jit(solution)/shard_map/ppermute | solution.py:32
  279.0 6.4 %collective-permute-start.21 = (f32[3,1,1,52,128]{4,3,2,1,0:T(8,128)S(1)}, f32[3,1,1,52,128]{4,3,2,1,0:T(8,128)S(1)}, u32[]{:S(2)}, u32[]{:S(2)}) collective-permute-start(f32[3,1,1,52,128]{4,3,2,1,0:T(8,128)S(1)} %pad_maximum_fusion.6), channel_id=1, source_target_pairs={{2,0},{4,2},{6,4},{3,1},{5,3},{7,5},{10,8},{12,10},{14,12},{11,9},... | collective-permute-start | bytes 239624 | tf_op jit(solution)/shard_map/ppermute | solution.py:34
  317.5 10.7 %collective-permute-start.24 = (f32[1,1,1,52,128]{4,3,2,1,0:T(8,128)S(1)}, f32[1,1,1,52,128]{4,3,2,1,0:T(8,128)S(1)}, u32[]{:S(2)}, u32[]{:S(2)}) collective-permute-start(f32[1,1,1,52,128]{4,3,2,1,0:T(8,128)S(1)} %bitcast.227), channel_id=1, source_target_pairs={{0,8},{8,16},{16,24},{1,9},{9,17},{17,25},{2,10},{10,18},{18,26},{... | collective-permute-start | bytes 79880 | tf_op jit(solution)/shard_map/ppermute | solution.py:32
  320.4 7.8 %collective-permute-start.25 = (f32[1,1,1,52,128]{4,3,2,1,0:T(8,128)S(1)}, f32[1,1,1,52,128]{4,3,2,1,0:T(8,128)S(1)}, u32[]{:S(2)}, u32[]{:S(2)}) collective-permute-start(f32[1,1,1,52,128]{4,3,2,1,0:T(8,128)S(1)} %bitcast.228), channel_id=1, source_target_pairs={{8,0},{16,8},{24,16},{9,1},{17,9},{25,17},{10,2},{18,10},{26,18},{... | collective-permute-start | bytes 79880 | tf_op jit(solution)/shard_map/ppermute | solution.py:34
  324.2 57.9 %collective-permute-start.50 = (f32[3,1,1,52,6,128]{5,2,4,3,1,0:T(1,128)}, f32[3,1,1,52,6,128]{5,2,4,3,1,0:T(1,128)}, u32[]{:S(2)}, u32[]{:S(2)}) collective-permute-start(f32[3,1,1,52,6,128]{5,2,4,3,1,0:T(1,128)} %copy.233), channel_id=1, source_target_pairs={{0,2},{2,4},{4,6},{1,3},{3,5},{5,7},{8,10},{10,12},{12,14},{9,11},... | collective-permute-start | bytes 1437704 | tf_op jit(solution)/shard_map/ppermute | solution.py:32
  326.9 56.3 %collective-permute-start.51 = (f32[3,1,1,52,6,128]{5,2,4,3,1,0:T(1,128)}, f32[3,1,1,52,6,128]{5,2,4,3,1,0:T(1,128)}, u32[]{:S(2)}, u32[]{:S(2)}) collective-permute-start(f32[3,1,1,52,6,128]{5,2,4,3,1,0:T(1,128)} %copy.233), channel_id=1, source_target_pairs={{2,0},{4,2},{6,4},{3,1},{5,3},{7,5},{10,8},{12,10},{14,12},{11,9},... | collective-permute-start | bytes 1437704 | tf_op jit(solution)/shard_map/ppermute | solution.py:34
  328.2 10.4 %collective-permute-start.26 = (f32[3,1,1,52,128]{4,3,2,1,0:T(8,128)S(1)}, f32[3,1,1,52,128]{4,3,2,1,0:T(8,128)S(1)}, u32[]{:S(2)}, u32[]{:S(2)}) collective-permute-start(f32[3,1,1,52,128]{4,3,2,1,0:T(8,128)S(1)} %pad_maximum_fusion.7), channel_id=1, source_target_pairs={{0,2},{2,4},{4,6},{1,3},{3,5},{5,7},{8,10},{10,12},{12,14},{9,11},... | collective-permute-start | bytes 239624 | tf_op jit(solution)/shard_map/ppermute | solution.py:32
  333.7 9.8 %collective-permute-start.27 = (f32[3,1,1,52,128]{4,3,2,1,0:T(8,128)S(1)}, f32[3,1,1,52,128]{4,3,2,1,0:T(8,128)S(1)}, u32[]{:S(2)}, u32[]{:S(2)}) collective-permute-start(f32[3,1,1,52,128]{4,3,2,1,0:T(8,128)S(1)} %pad_maximum_fusion.7), channel_id=1, source_target_pairs={{2,0},{4,2},{6,4},{3,1},{5,3},{7,5},{10,8},{12,10},{14,12},{11,9},... | collective-permute-start | bytes 239624 | tf_op jit(solution)/shard_map/ppermute | solution.py:34
  375.6 8.7 %collective-permute-start.30 = (f32[1,1,1,52,128]{4,3,2,1,0:T(8,128)S(1)}, f32[1,1,1,52,128]{4,3,2,1,0:T(8,128)S(1)}, u32[]{:S(2)}, u32[]{:S(2)}) collective-permute-start(f32[1,1,1,52,128]{4,3,2,1,0:T(8,128)S(1)} %bitcast.221), channel_id=1, source_target_pairs={{0,8},{8,16},{16,24},{1,9},{9,17},{17,25},{2,10},{10,18},{18,26},{... | collective-permute-start | bytes 79880 | tf_op jit(solution)/shard_map/ppermute | solution.py:32
  379.9 5.8 collective-permute-start.31
  385.7 10.4 %collective-permute-start.32 = (f32[3,1,1,52,128]{4,3,2,1,0:T(8,128)S(1)}, f32[3,1,1,52,128]{4,3,2,1,0:T(8,128)S(1)}, u32[]{:S(2)}, u32[]{:S(2)}) collective-permute-start(f32[3,1,1,52,128]{4,3,2,1,0:T(8,128)S(1)} %pad_maximum_fusion.8), channel_id=1, source_target_pairs={{0,2},{2,4},{4,6},{1,3},{3,5},{5,7},{8,10},{10,12},{12,14},{9,11},... | collective-permute-start | bytes 239624 | tf_op jit(solution)/shard_map/ppermute | solution.py:32
  391.1 53.9 %collective-permute-start.52 = (f32[3,3,1,52,6,128]{5,2,4,3,1,0:T(1,128)}, f32[3,3,1,52,6,128]{5,2,4,3,1,0:T(1,128)}, u32[]{:S(2)}, u32[]{:S(2)}) collective-permute-start(f32[3,3,1,52,6,128]{5,2,4,3,1,0:T(1,128)} %copy.239), channel_id=1, source_target_pairs={{0,1},{2,3},{4,5},{6,7},{8,9},{10,11},{12,13},{14,15},{16,17},{18,... | collective-permute-start | bytes 4313096 | tf_op jit(solution)/shard_map/ppermute | solution.py:32
  393.5 97.4 %collective-permute-start.53 = (f32[3,3,1,52,6,128]{5,2,4,3,1,0:T(1,128)}, f32[3,3,1,52,6,128]{5,2,4,3,1,0:T(1,128)}, u32[]{:S(2)}, u32[]{:S(2)}) collective-permute-start(f32[3,3,1,52,6,128]{5,2,4,3,1,0:T(1,128)} %copy.239), channel_id=1, source_target_pairs={{1,0},{3,2},{5,4},{7,6},{9,8},{11,10},{13,12},{15,14},{17,16},{19,... | collective-permute-start | bytes 4313096 | tf_op jit(solution)/shard_map/ppermute | solution.py:34
  394.8 6.4 %collective-permute-start.33 = (f32[3,1,1,52,128]{4,3,2,1,0:T(8,128)S(1)}, f32[3,1,1,52,128]{4,3,2,1,0:T(8,128)S(1)}, u32[]{:S(2)}, u32[]{:S(2)}) collective-permute-start(f32[3,1,1,52,128]{4,3,2,1,0:T(8,128)S(1)} %pad_maximum_fusion.8), channel_id=1, source_target_pairs={{2,0},{4,2},{6,4},{3,1},{5,3},{7,5},{10,8},{12,10},{14,12},{11,9},... | collective-permute-start | bytes 239624 | tf_op jit(solution)/shard_map/ppermute | solution.py:34
  401.2 4.6 collective-permute-start.35
  433.3 5.5 collective-permute-start.36
  437.3 5.8 collective-permute-start.37
  446.0 6.4 %collective-permute-start.39 = (f32[3,1,1,52,128]{4,3,2,1,0:T(8,128)S(1)}, f32[3,1,1,52,128]{4,3,2,1,0:T(8,128)S(1)}, u32[]{:S(2)}, u32[]{:S(2)}) collective-permute-start(f32[3,1,1,52,128]{4,3,2,1,0:T(8,128)S(1)} %pad_maximum_fusion.9), channel_id=1, source_target_pairs={{2,0},{4,2},{6,4},{3,1},{5,3},{7,5},{10,8},{12,10},{14,12},{11,9},... | collective-permute-start | bytes 239624 | tf_op jit(solution)/shard_map/ppermute | solution.py:34
  485.0 6.9 %collective-permute-start.42 = (f32[1,1,1,52,128]{4,3,2,1,0:T(8,128)S(1)}, f32[1,1,1,52,128]{4,3,2,1,0:T(8,128)S(1)}, u32[]{:S(2)}, u32[]{:S(2)}) collective-permute-start(f32[1,1,1,52,128]{4,3,2,1,0:T(8,128)S(1)} %bitcast.230), channel_id=1, source_target_pairs={{0,8},{8,16},{16,24},{1,9},{9,17},{17,25},{2,10},{10,18},{18,26},{... | collective-permute-start | bytes 79880 | tf_op jit(solution)/shard_map/ppermute | solution.py:32
  489.6 5.8 collective-permute-start.43
  495.4 5.7 collective-permute-start.44
  499.8 6.4 %collective-permute-start.45 = (f32[3,1,1,52,128]{4,3,2,1,0:T(8,128)S(1)}, f32[3,1,1,52,128]{4,3,2,1,0:T(8,128)S(1)}, u32[]{:S(2)}, u32[]{:S(2)}) collective-permute-start(f32[3,1,1,52,128]{4,3,2,1,0:T(8,128)S(1)} %pad_maximum_fusion.10), channel_id=1, source_target_pairs={{2,0},{4,2},{6,4},{3,1},{5,3},{7,5},{10,8},{12,10},{14,12},{11,9},... | collective-permute-start | bytes 239624 | tf_op jit(solution)/shard_map/ppermute | solution.py:34
  (16 other events, 115.3 us)
where the time goes:
time: 630 us; the launch traced here: 621 us
  matrix products  238 us (38%)
  starting transfers between devices  140 us (22%)
  blocking collectives  80.4 us (13%)
  waiting for transfers between devices  68.1 us (11%)
  local copies, waits for them, and re-layouts  62.8 us (10%)
  loops' own time  20.5 us (3%)
  other arithmetic  6.76 us (1%)
    dot_general x8, matrix products, local(): mixed = jnp.einsum('bkij,bkj->bi', a_blocks, picked, precision=precise_mode)  198 us
    ppermute x30, starting transfers between devices, with_halo(): lax.ppermute(tail, axis, [(i, (i + 1) % count) for i in range(ends)])  101 us
    ppermute x30, waiting for transfers between devices, with_halo(): lax.ppermute(head, axis, [((i + 1) % count, i) for i in range(ends)])  56.7 us
    unnamed x1, blocking collectives  42.3 us
    dot_general x1, matrix products, local(): jnp.einsum('bksj,bkij->bksi', picked_p0, a_blocks, precision=precise_mode)  40.1 us
    ppermute x30, starting transfers between devices, with_halo(): lax.ppermute(head, axis, [((i + 1) % count, i) for i in range(ends)])  38.9 us
    psum x1, blocking collectives, local(): lax.psum((jnp.sum(previous * previous), jnp.sum(current * current)), ('gx...  38.1 us
    another operation x1, loops' own time, carried_in(): return lax.fori_loop(0, count - 1, lap, so_far)  20.5 us
  transfers between devices with their start and end apart: 60, of which 26 were waited for; matrix products, arithmetic and copies ran while one was open for 38% of the time, Pallas kernels for 0%

commit v1 on v0

v1 whole, which is shorter than its diff:
```python
import jax
import jax.numpy as jnp
from jax import lax
from jax.experimental import pallas as pl
from jax.experimental.pallas import tpu as pltpu
from jax.sharding import PartitionSpec as P

ITERS = 8
AXES = ("gx", "gy", "gz")
MIB = 1 << 20
VMEM = pl.BlockSpec(memory_space=pltpu.VMEM)
SMEM = pl.BlockSpec(memory_space=pltpu.SMEM)
ANY = pl.BlockSpec(memory_space=pl.ANY)


def matchings(count):
    out = []
    for first in (0, 1):
        pairs = []
        for i in range(first, count - 1, 2):
            pairs += [(i, i + 1), (i + 1, i)]
        out.append(pairs)
    return out


def exchange(value):
    received, slots, used = [], [], 0
    for axis in AXES:
        mine = lax.axis_index(axis)
        base = used
        place = []
        for pairs in matchings(lax.axis_size(axis)):
            if pairs:
                received.append(lax.ppermute(value, axis, pairs))
                used += 1
            place.append(max(used, 1))
        even = (mine % 2) == 0
        slots.append(jnp.where(even, place[1], place[0]))
        slots.append(jnp.where(even, place[0], place[1]))
    return received, slots


def summed(value):
    for axis in reversed(AXES):
        count = lax.axis_size(axis)
        total = value
        for step in range(1, count):
            total = total + lax.ppermute(
                value, axis, [(i, (i + step) % count) for i in range(count)]
            )
        value = total
    return value


def split(value):
    high = value.astype(jnp.bfloat16)
    low = (value - high.astype(jnp.float32)).astype(jnp.bfloat16)
    return high, low


def dot_t(left, right):
    return lax.dot_general(
        left, right, (((1,), (1,)), ((), ())), preferred_element_type=jnp.float32
    )


def load_kernel(a_hbm, a_ref, sem):
    copy = pltpu.make_async_copy(a_hbm, a_ref, sem)
    copy.start()
    copy.wait()


def first_kernel(faces, index_ref, a_ref, *refs):
    own_ref, face_refs = refs[0], refs[1 : 1 + faces]
    prod_ref, z_ref, diag_ref, table = refs[1 + faces :]
    nb, nk, size, _ = a_ref.shape
    table[0:nb] = own_ref[...]
    for d in range(faces):
        table[(d + 1) * nb : (d + 2) * nb] = face_refs[d][...]
    sub = lax.broadcasted_iota(jnp.int32, (8, size), 0)

    def body(b, _):
        total = jnp.zeros((8, size), jnp.float32)
        for k in range(nk):
            block = a_ref[b, k]
            if k == 0:
                eye = lax.broadcasted_iota(jnp.int32, (size, size), 0) == (
                    lax.broadcasted_iota(jnp.int32, (size, size), 1)
                )
                diag = jnp.sum(jnp.where(eye, block, 0.0), axis=0, keepdims=True)
                diag_ref[pl.ds(b, 1), :] = diag
            rows = table[index_ref[b * nk + k]]
            rows_high, rows_low = split(rows)
            high, low = split(block)
            product = dot_t(rows_high, high) + (dot_t(rows_low, high) + dot_t(rows_high, low))
            total = total + product
            prod_ref[b * nk + k] = jnp.where(sub == 7, rows, product)
        z_ref[pl.ds(b, 1), :] = total[0:1, :] / diag
        return 0

    lax.fori_loop(0, nb, body, 0)


def step_kernel(faces, last, index_ref, a_ref, *refs):
    own_ref, face_refs = refs[0], refs[1 : 1 + faces]
    diag_ref = refs[1 + faces]
    outs = refs[2 + faces :]
    z_ref, table = outs[0], outs[-1]
    nb, nk, size, _ = a_ref.shape
    stride = table.shape[0] // (faces + 1)
    table[0:nb, :] = own_ref[...]
    for d in range(faces):
        table[(d + 1) * stride : (d + 1) * stride + nb, :] = face_refs[d][...]
    ones = jnp.ones((8, size), jnp.bfloat16)

    def body(b, _):
        acc = None
        for k in range(nk):
            term = a_ref[b, k] * table[pl.ds(index_ref[b * nk + k], 1), :]
            acc = term if acc is None else acc + term
        high, low = split(acc)
        row = dot_t(ones, high) + dot_t(ones, low)
        z_ref[pl.ds(b, 1), :] = row[0:1, :] / diag_ref[pl.ds(b, 1), :]
        return 0

    lax.fori_loop(0, nb, body, 0, unroll=2 if nb % 2 == 0 else 1)
    if last:
        before, now = own_ref[...], z_ref[...]
        outs[1][0:1, :] = jnp.sum(before * before, axis=0, keepdims=True)
        outs[1][1:2, :] = jnp.sum(now * now, axis=0, keepdims=True)


def final_kernel(root_total, ids_ref, totals_ref, cols_ref, prod_ref, x_ref, diag_ref, z_ref, *outs):
    p_ref, c_ref, power_ref = outs
    nk, ns, nb, size = p_ref.shape
    totals = totals_ref[...]
    last_norm = jnp.sqrt(totals[:, 1:2])
    spectral = last_norm / jnp.sqrt(totals[:, 0:1])
    damping = 4.0 / (3.0 * spectral)
    power_ref[...] = z_ref[...] * (root_total / last_norm)
    lane = lax.broadcasted_iota(jnp.int32, totals.shape, 1) - 2
    offsets = [
        jnp.sum(
            jnp.where((lane >= 0) & (lane < ids_ref[d]), totals, 0.0), axis=1, keepdims=True
        )
        for d in range(7)
    ]
    for start in range(0, nb, 8):
        n = min(8, nb - start)
        scale = damping / diag_ref[start : start + n, :]
        cols = cols_ref[start : start + n, :]
        base = jnp.broadcast_to(offsets[0], cols.shape)
        for d in range(1, 7):
            base = jnp.where(cols >= d * nb, offsets[d], base)
        column = lax.broadcasted_iota(jnp.int32, cols.shape, 1)
        for k in range(nk):
            at = (start * nk + k) * 8
            for s in range(ns):
                value = -scale * prod_ref[pl.ds(at + s + 1, n, stride=nk * 8), :]
                if k == 0:
                    value = value + x_ref[pl.ds(start * 8 + s + 1, n, stride=8), :]
                p_ref[k, s, start : start + n, :] = value
            names = prod_ref[pl.ds(at + 7, n, stride=nk * 8), :]
            base = base + jnp.where(column == k, names[:, : cols.shape[1]], 0.0)
        c_ref[start : start + n, :] = ns * base.astype(jnp.int32)


def call(kernel, out_shape, in_specs, scratch=(), limit=34 * MIB):
    many = isinstance(out_shape, (tuple, list))
    return pl.pallas_call(
        kernel,
        out_shape=out_shape,
        in_specs=in_specs,
        out_specs=tuple(VMEM for _ in out_shape) if many else VMEM,
        scratch_shapes=list(scratch),
        compiler_params=pltpu.CompilerParams(vmem_limit_bytes=limit),
    )


def local(a_blocks, block_cols, agg_ids, agg_counts, p0_blocks, start_vec):
    nb, nk, size, _ = a_blocks.shape
    ns = p0_blocks.shape[1]
    f32 = jnp.float32
    devices = 1
    me = jnp.int32(0)
    for axis in AXES:
        devices *= lax.axis_size(axis)
        me = me * lax.axis_size(axis) + lax.axis_index(axis)
    strides = (lax.axis_size("gy") * lax.axis_size("gz"), lax.axis_size("gz"), 1)
    ids = jnp.stack([me] + [me + sign * s for s in strides for sign in (-1, 1)])

    a_here = call(
        load_kernel,
        pltpu.VMEM(a_blocks.shape, f32),
        [ANY],
        [pltpu.SemaphoreType.DMA],
    )(a_blocks)

    names = jnp.broadcast_to(agg_ids.astype(f32)[:, None, None], (nb, 1, size))
    x_own = jnp.concatenate([start_vec[:, None, :], p0_blocks, names], axis=1)
    x_faces, slots = exchange(x_own)
    faces = len(x_faces)
    way = block_cols // nb
    slot = jnp.zeros_like(block_cols)
    for d in range(6):
        slot = jnp.where(way == d + 1, slots[d], slot)
    row = block_cols - way * nb
    stride = -(-nb // 8) * 8
    first_index = (slot * nb + row).reshape(-1)
    index = (slot * stride + row).reshape(-1)

    prod, current, diag = call(
        lambda *r: first_kernel(faces, *r),
        (
            jax.ShapeDtypeStruct((nb * nk, 8, size), f32),
            jax.ShapeDtypeStruct((nb, size), f32),
            jax.ShapeDtypeStruct((nb, size), f32),
        ),
        [SMEM, VMEM, VMEM] + [VMEM] * faces,
        [pltpu.VMEM(((faces + 1) * nb, 8, size), f32)],
    )(first_index, a_here, x_own, *x_faces)

    for turn in range(1, ITERS):
        last = turn == ITERS - 1
        received, _ = exchange(current)
        shapes = [jax.ShapeDtypeStruct((nb, size), f32)]
        if last:
            shapes.append(jax.ShapeDtypeStruct((2, size), f32))
        results = call(
            lambda *r, last=last: step_kernel(faces, last, *r),
            tuple(shapes),
            [SMEM, VMEM, VMEM] + [VMEM] * faces + [VMEM],
            [pltpu.VMEM(((faces + 1) * stride, size), f32)],
        )(index, a_here, current, *received, diag)
        current = results[0]

    mark = jnp.where(jnp.arange(devices) == me, agg_counts[0].astype(f32), 0.0)
    totals = summed(jnp.concatenate([jnp.sum(results[1], axis=1), mark])[None, :])

    smoothed, p_cols, power_vec = call(
        lambda *r: final_kernel(float((devices * nb * size) ** 0.5), *r),
        (
            jax.ShapeDtypeStruct((nk, ns, nb, size), f32),
            jax.ShapeDtypeStruct((nb, nk), jnp.int32),
            jax.ShapeDtypeStruct((nb, size), f32),
        ),
        [SMEM] + [VMEM] * 6,
    )(
        ids,
        totals,
        block_cols,
        prod.reshape(nb * nk * 8, size),
        x_own.reshape(nb * 8, size),
        diag,
        current,
    )
    return jnp.transpose(smoothed, (2, 0, 1, 3)), p_cols, power_vec


def solution(mesh):
    spec = P(AXES)
    return jax.shard_map(
        local, mesh=mesh, in_specs=(spec,) * 6, out_specs=(spec,) * 3, check_vma=False
    )
```

time: 630 us -> 254 us (0.40); the launches traced: 621 us -> 253 us
  matrix products: 238 us -> 0 us
  Pallas kernels: 0 us -> 141 us
  blocking collectives: 80.4 us -> 0 us
  starting transfers between devices: 140 us -> 74 us
  local copies, waits for them, and re-layouts: 62.8 us -> 11 us
  waiting for transfers between devices: 68.1 us -> 22.9 us
  loops' own time: 20.5 us -> 0 us
    dot_general x9 -> x0, matrix products: 238 us -> none  [the longest x8 198 us: local(): mixed = jnp.einsum('bkij,bkj->bi', a_blocks, picked, precision=precise_mode)]
    pallas_call x0 -> x10, Pallas kernels: none -> 141 us  [the longest x7 98 us: local(): call(lambda *r, last=last: step_kernel(faces, last, *r), tuple(shapes), [...]
    ppermute x60 -> x47, starting transfers between devices: 140 us -> 74 us  [the longest x40 67.3 us: exchange(): received.append(lax.ppermute(value, axis, pairs))]
    ppermute x60 -> x47, waiting for transfers between devices: 68.1 us -> 22.9 us  [the longest x40 13.3 us: exchange(): received.append(lax.ppermute(value, axis, pairs))]
    unnamed x1 -> x0, blocking collectives: 42.3 us -> none
    psum x1 -> x0, blocking collectives: 38.1 us -> none  [local(): lax.psum((jnp.sum(previous * previous), jnp.sum(current * current)), ('gx...]
    another operation x1 -> x0, loops' own time: 20.5 us -> none  [carried_in(): return lax.fori_loop(0, count - 1, lap, so_far)]
    dynamic_slice x31 -> x0, local copies, waits for them, and re-layouts: 19 us -> none  [lap(): longer = join(so_far, pieces[position])]
  transfers between devices with their start and end apart: 60 -> 47, of which waited for: 26 -> 13; matrix products, arithmetic and copies ran while one was open for 38% -> 1% of each run, Pallas kernels for 0% -> 3%
where the time goes in v1:
time: 254 us; the launch traced here: 253 us
  Pallas kernels  141 us (56%)
  starting transfers between devices  74 us (29%)
  waiting for transfers between devices  22.9 us (9%)
  local copies, waits for them, and re-layouts  11 us (4%)
    pallas_call x7, Pallas kernels, local(): call(lambda *r, last=last: step_kernel(faces, last, *r), tuple(shapes), [...  98 us
    ppermute x40, starting transfers between devices, exchange(): received.append(lax.ppermute(value, axis, pairs))  67.3 us
    pallas_call x1, Pallas kernels, local(): call(lambda *r: first_kernel(faces, *r), (jax.ShapeDtypeStruct((nb * nk,...  33.4 us
    ppermute x40, waiting for transfers between devices, exchange(): received.append(lax.ppermute(value, axis, pairs))  13.3 us
    ppermute x7, waiting for transfers between devices, summed(): lax.ppermute(value, axis, [(i, (i + step) % count) for i in range(count)])  9.68 us
    unnamed x7, local copies, waits for them, and re-layouts  9.6 us
    pallas_call x1, Pallas kernels, local(): call(load_kernel, pltpu.VMEM(a_blocks.shape, f32), [ANY], [pltpu.Semaphor...  7.8 us
    ppermute x7, starting transfers between devices, summed(): lax.ppermute(value, axis, [(i, (i + step) % count) for i in range(count)])  6.68 us
  transfers between devices with their start and end apart: 47, of which 13 were waited for; matrix products, arithmetic and copies ran while one was open for 1% of the time, Pallas kernels for 3%

profile of v1, /device:TPU:0, one launch (start us, length us, event | category | flops | bytes accessed | tf_op | source)
XLA Modules:
  0.0 252.6 jit_solution(17789173080229196501)
XLA Ops:
  1.3 0.8 broadcast_in_dim.43
  2.1 1.0 copy.14
  4.5 5.5 %collective-permute-start.2 = (f32[52,8,128]{2,1,0:T(8,128)S(1)}, f32[52,8,128]{2,1,0:T(8,128)S(1)}, u32[]{:S(2)}, u32[]{:S(2)}) collective-permute-start(f32[52,8,128]{2,1,0:T(8,128)S(1)} %pad_maximum_fusion.r_2_), channel_id=1, source_target_pairs={{0,2},{2,0},{4,6},{6,4},{1,3},{3,1},{5,7},{7,5},{8,10},{10,8},{12,... | collective-permute-start | bytes 638984 | tf_op jit(solution)/shard_map/ppermute | solution.py:34
  10.6 4.3 %collective-permute-start = (f32[52,8,128]{2,1,0:T(8,128)S(1)}, f32[52,8,128]{2,1,0:T(8,128)S(1)}, u32[]{:S(2)}, u32[]{:S(2)}) collective-permute-start(f32[52,8,128]{2,1,0:T(8,128)S(1)} %pad_maximum_fusion.r_2_), channel_id=1, source_target_pairs={{0,8},{8,0},{16,24},{24,16},{1,9},{9,1},{17,25},{25,17},{2,10},{10... | collective-permute-start | bytes 638984 | tf_op jit(solution)/shard_map/ppermute | solution.py:34
  14.9 0.7 multiply_add_fusion
  15.8 7.8 %shard_map.85.r_1_ = f32[52,7,128,128]{3,2,1,0:T(8,128)S(1)} custom-call(f32[52,7,128,128]{3,2,1,0:T(8,128)} %a_hbm.1), custom_call_target="tpu_custom_call" | custom-call | tf_op jit(solution)/shard_map/pallas_call | solution.py:192
  23.6 7.9 %copy-done = f32[52,7,128,128]{3,2,1,0:T(8,128)} copy-done((f32[52,7,128,128]{3,2,1,0:T(8,128)}, f32[52,7,128,128]{3,2,1,0:T(8,128)S(1)}, u32[]{:S(2)}) %copy-start) | copy-done | bytes 23855128
  31.5 33.4 %shard_map.86 = (f32[364,8,128]{2,1,0:T(8,128)S(1)}, f32[52,128]{1,0:T(8,128)S(1)}, f32[52,128]{1,0:T(8,128)S(1)}) custom-call(s32[364]{0:T(512)S(1)} %reshape.23.r_0_, f32[52,7,128,128]{3,2,1,0:T(8,128)} %copy-done, f32[52,8,128]{2,1,0:T(8,128)S(1)} %pad_maximum_fusion.r_2_, f32[52,8,128]{2,1,0:T(8,128)S(1)} %collective-permute-done.r_3_, ...), custom_call_target="tpu_custom_call" | custom-call | tf_op jit(solution)/shard_map/pallas_call | solution.py:212
  65.6 1.8 collective-permute-start.7
  68.1 2.8 %collective-permute-start.5 = (f32[52,128]{1,0:T(8,128)S(1)}, f32[52,128]{1,0:T(8,128)S(1)}, u32[]{:S(2)}, u32[]{:S(2)}) collective-permute-start(f32[52,128]{1,0:T(8,128)S(1)} %get-tuple-element.11.r_2_), channel_id=1, source_target_pairs={{0,8},{8,0},{16,24},{24,16},{1,9},{9,1},{17,25},{25,17},{2,10},{10... | collective-permute-start | bytes 79880 | tf_op jit(solution)/shard_map/ppermute | solution.py:34
  71.2 1.8 collective-permute-done.5.r_3_
  73.0 14.0 %shard_map.87.r_2_ = f32[52,128]{1,0:T(8,128)S(1)} custom-call(s32[364]{0:T(512)S(1)} %reshape.22.r_0_, f32[52,7,128,128]{3,2,1,0:T(8,128)} %copy-done, f32[52,128]{1,0:T(8,128)S(1)} %get-tuple-element.11.r_2_, f32[52,128]{1,0:T(8,128)S(1)} %collective-permute-done.5.r_3_, f32[52,128]{1,0:T(8,128)S(1)} %collective-permute-done.6.r_4_, ...), custom_call_target="tpu_custom_call" | custom-call | tf_op jit(solution)/shard_map/pallas_call | solution.py:229
  87.6 2.9 %collective-permute-start.12 = (f32[52,128]{1,0:T(8,128)S(1)}, f32[52,128]{1,0:T(8,128)S(1)}, u32[]{:S(2)}, u32[]{:S(2)}) collective-permute-start(f32[52,128]{1,0:T(8,128)S(1)} %shard_map.87.r_2_), channel_id=1, source_target_pairs={{0,2},{2,0},{4,6},{6,4},{1,3},{3,1},{5,7},{7,5},{8,10},{10,8},{12,... | collective-permute-start | bytes 79880 | tf_op jit(solution)/shard_map/ppermute | solution.py:34
  91.2 4.6 %collective-permute-start.10 = (f32[52,128]{1,0:T(8,128)S(1)}, f32[52,128]{1,0:T(8,128)S(1)}, u32[]{:S(2)}, u32[]{:S(2)}) collective-permute-start(f32[52,128]{1,0:T(8,128)S(1)} %shard_map.87.r_2_), channel_id=1, source_target_pairs={{0,8},{8,0},{16,24},{24,16},{1,9},{9,1},{17,25},{25,17},{2,10},{10... | collective-permute-start | bytes 79880 | tf_op jit(solution)/shard_map/ppermute | solution.py:34
  95.8 2.0 collective-permute-done.10.r_3_
  97.9 14.0 %shard_map.88.r_2_ = f32[52,128]{1,0:T(8,128)S(1)} custom-call(s32[364]{0:T(512)S(1)} %reshape.22.r_0_, f32[52,7,128,128]{3,2,1,0:T(8,128)} %copy-done, f32[52,128]{1,0:T(8,128)S(1)} %shard_map.87.r_2_, f32[52,128]{1,0:T(8,128)S(1)} %collective-permute-done.10.r_3_, f32[52,128]{1,0:T(8,128)S(1)} %collective-permute-done.11.r_4_, ...), custom_call_target="tpu_custom_call" | custom-call | tf_op jit(solution)/shard_map/pallas_call | solution.py:229
  111.9 0.7 collective-permute-start.18
  112.5 2.1 collective-permute-start.17
  115.3 4.5 %collective-permute-start.15 = (f32[52,128]{1,0:T(8,128)S(1)}, f32[52,128]{1,0:T(8,128)S(1)}, u32[]{:S(2)}, u32[]{:S(2)}) collective-permute-start(f32[52,128]{1,0:T(8,128)S(1)} %shard_map.88.r_2_), channel_id=1, source_target_pairs={{0,8},{8,0},{16,24},{24,16},{1,9},{9,1},{17,25},{25,17},{2,10},{10... | collective-permute-start | bytes 79880 | tf_op jit(solution)/shard_map/ppermute | solution.py:34
  119.8 2.0 collective-permute-done.15.r_3_
  121.9 14.0 %shard_map.89.r_2_ = f32[52,128]{1,0:T(8,128)S(1)} custom-call(s32[364]{0:T(512)S(1)} %reshape.22.r_0_, f32[52,7,128,128]{3,2,1,0:T(8,128)} %copy-done, f32[52,128]{1,0:T(8,128)S(1)} %shard_map.88.r_2_, f32[52,128]{1,0:T(8,128)S(1)} %collective-permute-done.15.r_3_, f32[52,128]{1,0:T(8,128)S(1)} %collective-permute-done.16.r_4_, ...), custom_call_target="tpu_custom_call" | custom-call | tf_op jit(solution)/shard_map/pallas_call | solution.py:229
  135.9 0.7 collective-permute-start.23
  136.6 2.6 %collective-permute-start.22 = (f32[52,128]{1,0:T(8,128)S(1)}, f32[52,128]{1,0:T(8,128)S(1)}, u32[]{:S(2)}, u32[]{:S(2)}) collective-permute-start(f32[52,128]{1,0:T(8,128)S(1)} %shard_map.89.r_2_), channel_id=1, source_target_pairs={{0,2},{2,0},{4,6},{6,4},{1,3},{3,1},{5,7},{7,5},{8,10},{10,8},{12,... | collective-permute-start | bytes 79880 | tf_op jit(solution)/shard_map/ppermute | solution.py:34
  139.8 4.6 %collective-permute-start.20 = (f32[52,128]{1,0:T(8,128)S(1)}, f32[52,128]{1,0:T(8,128)S(1)}, u32[]{:S(2)}, u32[]{:S(2)}) collective-permute-start(f32[52,128]{1,0:T(8,128)S(1)} %shard_map.89.r_2_), channel_id=1, source_target_pairs={{0,8},{8,0},{16,24},{24,16},{1,9},{9,1},{17,25},{25,17},{2,10},{10... | collective-permute-start | bytes 79880 | tf_op jit(solution)/shard_map/ppermute | solution.py:34
  144.5 2.0 collective-permute-done.20.r_3_
  146.5 14.0 %shard_map.90.r_2_ = f32[52,128]{1,0:T(8,128)S(1)} custom-call(s32[364]{0:T(512)S(1)} %reshape.22.r_0_, f32[52,7,128,128]{3,2,1,0:T(8,128)} %copy-done, f32[52,128]{1,0:T(8,128)S(1)} %shard_map.89.r_2_, f32[52,128]{1,0:T(8,128)S(1)} %collective-permute-done.20.r_3_, f32[52,128]{1,0:T(8,128)S(1)} %collective-permute-done.21.r_4_, ...), custom_call_target="tpu_custom_call" | custom-call | tf_op jit(solution)/shard_map/pallas_call | solution.py:229
  161.2 2.1 collective-permute-start.27
  163.9 4.5 %collective-permute-start.25 = (f32[52,128]{1,0:T(8,128)S(1)}, f32[52,128]{1,0:T(8,128)S(1)}, u32[]{:S(2)}, u32[]{:S(2)}) collective-permute-start(f32[52,128]{1,0:T(8,128)S(1)} %shard_map.90.r_2_), channel_id=1, source_target_pairs={{0,8},{8,0},{16,24},{24,16},{1,9},{9,1},{17,25},{25,17},{2,10},{10... | collective-permute-start | bytes 79880 | tf_op jit(solution)/shard_map/ppermute | solution.py:34
  168.5 2.0 collective-permute-done.25.r_3_
  170.5 14.0 %shard_map.91.r_2_ = f32[52,128]{1,0:T(8,128)S(1)} custom-call(s32[364]{0:T(512)S(1)} %reshape.22.r_0_, f32[52,7,128,128]{3,2,1,0:T(8,128)} %copy-done, f32[52,128]{1,0:T(8,128)S(1)} %shard_map.90.r_2_, f32[52,128]{1,0:T(8,128)S(1)} %collective-permute-done.25.r_3_, f32[52,128]{1,0:T(8,128)S(1)} %collective-permute-done.26.r_4_, ...), custom_call_target="tpu_custom_call" | custom-call | tf_op jit(solution)/shard_map/pallas_call | solution.py:229
  185.2 2.6 %collective-permute-start.32 = (f32[52,128]{1,0:T(8,128)S(1)}, f32[52,128]{1,0:T(8,128)S(1)}, u32[]{:S(2)}, u32[]{:S(2)}) collective-permute-start(f32[52,128]{1,0:T(8,128)S(1)} %shard_map.91.r_2_), channel_id=1, source_target_pairs={{0,2},{2,0},{4,6},{6,4},{1,3},{3,1},{5,7},{7,5},{8,10},{10,8},{12,... | collective-permute-start | bytes 79880 | tf_op jit(solution)/shard_map/ppermute | solution.py:34
  188.5 4.6 %collective-permute-start.30 = (f32[52,128]{1,0:T(8,128)S(1)}, f32[52,128]{1,0:T(8,128)S(1)}, u32[]{:S(2)}, u32[]{:S(2)}) collective-permute-start(f32[52,128]{1,0:T(8,128)S(1)} %shard_map.91.r_2_), channel_id=1, source_target_pairs={{0,8},{8,0},{16,24},{24,16},{1,9},{9,1},{17,25},{25,17},{2,10},{10... | collective-permute-start | bytes 79880 | tf_op jit(solution)/shard_map/ppermute | solution.py:34
  193.9 1.3 collective-permute-done.30.r_3_
  195.2 14.0 %shard_map.92.r_2_ = f32[52,128]{1,0:T(8,128)S(1)} custom-call(s32[364]{0:T(512)S(1)} %reshape.22.r_0_, f32[52,7,128,128]{3,2,1,0:T(8,128)} %copy-done, f32[52,128]{1,0:T(8,128)S(1)} %shard_map.91.r_2_, f32[52,128]{1,0:T(8,128)S(1)} %collective-permute-done.30.r_3_, f32[52,128]{1,0:T(8,128)S(1)} %collective-permute-done.31.r_4_, ...), custom_call_target="tpu_custom_call" | custom-call | tf_op jit(solution)/shard_map/pallas_call | solution.py:229
  209.8 2.1 collective-permute-start.37
  212.6 4.5 %collective-permute-start.35 = (f32[52,128]{1,0:T(8,128)S(1)}, f32[52,128]{1,0:T(8,128)S(1)}, u32[]{:S(2)}, u32[]{:S(2)}) collective-permute-start(f32[52,128]{1,0:T(8,128)S(1)} %shard_map.92.r_2_), channel_id=1, source_target_pairs={{0,8},{8,0},{16,24},{24,16},{1,9},{9,1},{17,25},{25,17},{2,10},{10... | collective-permute-start | bytes 79880 | tf_op jit(solution)/shard_map/ppermute | solution.py:34
  217.2 1.9 collective-permute-done.35.r_3_
  219.2 14.0 %shard_map.93 = (f32[52,128]{1,0:T(8,128)S(1)}, f32[2,128]{1,0:T(2,128)S(1)}) custom-call(s32[364]{0:T(512)S(1)} %reshape.22.r_0_, f32[52,7,128,128]{3,2,1,0:T(8,128)} %copy-done, f32[52,128]{1,0:T(8,128)S(1)} %shard_map.92.r_2_, f32[52,128]{1,0:T(8,128)S(1)} %collective-permute-done.35.r_3_, f32[52,128]{1,0:T(8,128)S(1)} %collective-permute-done.36.r_4_, ...), custom_call_target="tpu_custom_call" | custom-call | tf_op jit(solution)/shard_map/pallas_call | solution.py:229
  233.5 1.1 collective-permute-done.40
  234.6 2.2 collective-permute-start.43
  237.5 0.7 collective-permute-done.43
  238.2 3.1 %collective-permute-done.42 = f32[1,34]{1,0:T(1,128)S(1)} collective-permute-done((f32[1,34]{1,0:T(1,128)S(1)}, f32[1,34]{1,0:T(1,128)S(1)}, u32[]{:S(2)}, u32[]{:S(2)}) %collective-permute-start.42) | collective-permute-done | bytes 168 | tf_op jit(solution)/shard_map/ppermute | solution.py:48
  241.3 0.9 collective-permute-done.41
  242.2 1.5 collective-permute-start.46
  243.7 1.8 collective-permute-start.45
  246.1 1.2 collective-permute-done.45
  247.3 2.7 %collective-permute-done.44 = f32[1,34]{1,0:T(1,128)S(1)} collective-permute-done((f32[1,34]{1,0:T(1,128)S(1)}, f32[1,34]{1,0:T(1,128)S(1)}, u32[]{:S(2)}, u32[]{:S(2)}) %collective-permute-start.44) | collective-permute-done | bytes 168 | tf_op jit(solution)/shard_map/ppermute | solution.py:48
  250.0 2.0 shard_map.94
  (80 shorter events, 13.7 us)
Async XLA Ops:
  3.2 28.3 %collective-permute-start.4 = (f32[52,8,128]{2,1,0:T(8,128)S(1)}, f32[52,8,128]{2,1,0:T(8,128)S(1)}, u32[]{:S(2)}, u32[]{:S(2)}) collective-permute-start(f32[52,8,128]{2,1,0:T(8,128)S(1)} %pad_maximum_fusion.r_2_), channel_id=1, source_target_pairs={{0,1},{1,0},{2,3},{3,2},{4,5},{5,4},{6,7},{7,6},{8,9},{9,8},{10,11... | collective-permute-start | bytes 638984 | tf_op jit(solution)/shard_map/ppermute | solution.py:34
  3.8 27.7 %collective-permute-start.3 = (f32[52,8,128]{2,1,0:T(8,128)S(1)}, f32[52,8,128]{2,1,0:T(8,128)S(1)}, u32[]{:S(2)}, u32[]{:S(2)}) collective-permute-start(f32[52,8,128]{2,1,0:T(8,128)S(1)} %pad_maximum_fusion.r_2_), channel_id=1, source_target_pairs={{2,4},{4,2},{3,5},{5,3},{10,12},{12,10},{11,13},{13,11},{18,20},{2... | collective-permute-start | bytes 638984 | tf_op jit(solution)/shard_map/ppermute | solution.py:34
  4.5 27.0 %collective-permute-start.2 = (f32[52,8,128]{2,1,0:T(8,128)S(1)}, f32[52,8,128]{2,1,0:T(8,128)S(1)}, u32[]{:S(2)}, u32[]{:S(2)}) collective-permute-start(f32[52,8,128]{2,1,0:T(8,128)S(1)} %pad_maximum_fusion.r_2_), channel_id=1, source_target_pairs={{0,2},{2,0},{4,6},{6,4},{1,3},{3,1},{5,7},{7,5},{8,10},{10,8},{12,... | collective-permute-start | bytes 638984 | tf_op jit(solution)/shard_map/ppermute | solution.py:34
  9.9 21.6 %collective-permute-start.1 = (f32[52,8,128]{2,1,0:T(8,128)S(1)}, f32[52,8,128]{2,1,0:T(8,128)S(1)}, u32[]{:S(2)}, u32[]{:S(2)}) collective-permute-start(f32[52,8,128]{2,1,0:T(8,128)S(1)} %pad_maximum_fusion.r_2_), channel_id=1, source_target_pairs={{8,16},{16,8},{9,17},{17,9},{10,18},{18,10},{11,19},{19,11},{12,20... | collective-permute-start | bytes 638984 | tf_op jit(solution)/shard_map/ppermute | solution.py:34
  10.6 20.9 %collective-permute-start = (f32[52,8,128]{2,1,0:T(8,128)S(1)}, f32[52,8,128]{2,1,0:T(8,128)S(1)}, u32[]{:S(2)}, u32[]{:S(2)}) collective-permute-start(f32[52,8,128]{2,1,0:T(8,128)S(1)} %pad_maximum_fusion.r_2_), channel_id=1, source_target_pairs={{0,8},{8,0},{16,24},{24,16},{1,9},{9,1},{17,25},{25,17},{2,10},{10... | collective-permute-start | bytes 638984 | tf_op jit(solution)/shard_map/ppermute | solution.py:34
  65.0 6.2 %collective-permute-start.9 = (f32[52,128]{1,0:T(8,128)S(1)}, f32[52,128]{1,0:T(8,128)S(1)}, u32[]{:S(2)}, u32[]{:S(2)}) collective-permute-start(f32[52,128]{1,0:T(8,128)S(1)} %get-tuple-element.11.r_2_), channel_id=1, source_target_pairs={{0,1},{1,0},{2,3},{3,2},{4,5},{5,4},{6,7},{7,6},{8,9},{9,8},{10,11... | collective-permute-start | bytes 79880 | tf_op jit(solution)/shard_map/ppermute | solution.py:34
  65.0 6.2 %collective-permute-start.8 = (f32[52,128]{1,0:T(8,128)S(1)}, f32[52,128]{1,0:T(8,128)S(1)}, u32[]{:S(2)}, u32[]{:S(2)}) collective-permute-start(f32[52,128]{1,0:T(8,128)S(1)} %get-tuple-element.11.r_2_), channel_id=1, source_target_pairs={{2,4},{4,2},{3,5},{5,3},{10,12},{12,10},{11,13},{13,11},{18,20},{2... | collective-permute-start | bytes 79880 | tf_op jit(solution)/shard_map/ppermute | solution.py:34
  65.6 5.5 %collective-permute-start.7 = (f32[52,128]{1,0:T(8,128)S(1)}, f32[52,128]{1,0:T(8,128)S(1)}, u32[]{:S(2)}, u32[]{:S(2)}) collective-permute-start(f32[52,128]{1,0:T(8,128)S(1)} %get-tuple-element.11.r_2_), channel_id=1, source_target_pairs={{0,2},{2,0},{4,6},{6,4},{1,3},{3,1},{5,7},{7,5},{8,10},{10,8},{12,... | collective-permute-start | bytes 79880 | tf_op jit(solution)/shard_map/ppermute | solution.py:34
  67.4 3.7 %collective-permute-start.6 = (f32[52,128]{1,0:T(8,128)S(1)}, f32[52,128]{1,0:T(8,128)S(1)}, u32[]{:S(2)}, u32[]{:S(2)}) collective-permute-start(f32[52,128]{1,0:T(8,128)S(1)} %get-tuple-element.11.r_2_), channel_id=1, source_target_pairs={{8,16},{16,8},{9,17},{17,9},{10,18},{18,10},{11,19},{19,11},{12,20... | collective-permute-start | bytes 79880 | tf_op jit(solution)/shard_map/ppermute | solution.py:34
  68.1 4.9 %collective-permute-start.5 = (f32[52,128]{1,0:T(8,128)S(1)}, f32[52,128]{1,0:T(8,128)S(1)}, u32[]{:S(2)}, u32[]{:S(2)}) collective-permute-start(f32[52,128]{1,0:T(8,128)S(1)} %get-tuple-element.11.r_2_), channel_id=1, source_target_pairs={{0,8},{8,0},{16,24},{24,16},{1,9},{9,1},{17,25},{25,17},{2,10},{10... | collective-permute-start | bytes 79880 | tf_op jit(solution)/shard_map/ppermute | solution.py:34
  86.9 8.9 %collective-permute-start.14 = (f32[52,128]{1,0:T(8,128)S(1)}, f32[52,128]{1,0:T(8,128)S(1)}, u32[]{:S(2)}, u32[]{:S(2)}) collective-permute-start(f32[52,128]{1,0:T(8,128)S(1)} %shard_map.87.r_2_), channel_id=1, source_target_pairs={{0,1},{1,0},{2,3},{3,2},{4,5},{5,4},{6,7},{7,6},{8,9},{9,8},{10,11... | collective-permute-start | bytes 79880 | tf_op jit(solution)/shard_map/ppermute | solution.py:34
  86.9 8.9 %collective-permute-start.13 = (f32[52,128]{1,0:T(8,128)S(1)}, f32[52,128]{1,0:T(8,128)S(1)}, u32[]{:S(2)}, u32[]{:S(2)}) collective-permute-start(f32[52,128]{1,0:T(8,128)S(1)} %shard_map.87.r_2_), channel_id=1, source_target_pairs={{2,4},{4,2},{3,5},{5,3},{10,12},{12,10},{11,13},{13,11},{18,20},{2... | collective-permute-start | bytes 79880 | tf_op jit(solution)/shard_map/ppermute | solution.py:34
  87.6 8.2 %collective-permute-start.12 = (f32[52,128]{1,0:T(8,128)S(1)}, f32[52,128]{1,0:T(8,128)S(1)}, u32[]{:S(2)}, u32[]{:S(2)}) collective-permute-start(f32[52,128]{1,0:T(8,128)S(1)} %shard_map.87.r_2_), channel_id=1, source_target_pairs={{0,2},{2,0},{4,6},{6,4},{1,3},{3,1},{5,7},{7,5},{8,10},{10,8},{12,... | collective-permute-start | bytes 79880 | tf_op jit(solution)/shard_map/ppermute | solution.py:34
  90.5 5.3 %collective-permute-start.11 = (f32[52,128]{1,0:T(8,128)S(1)}, f32[52,128]{1,0:T(8,128)S(1)}, u32[]{:S(2)}, u32[]{:S(2)}) collective-permute-start(f32[52,128]{1,0:T(8,128)S(1)} %shard_map.87.r_2_), channel_id=1, source_target_pairs={{8,16},{16,8},{9,17},{17,9},{10,18},{18,10},{11,19},{19,11},{12,20... | collective-permute-start | bytes 79880 | tf_op jit(solution)/shard_map/ppermute | solution.py:34
  91.2 6.7 %collective-permute-start.10 = (f32[52,128]{1,0:T(8,128)S(1)}, f32[52,128]{1,0:T(8,128)S(1)}, u32[]{:S(2)}, u32[]{:S(2)}) collective-permute-start(f32[52,128]{1,0:T(8,128)S(1)} %shard_map.87.r_2_), channel_id=1, source_target_pairs={{0,8},{8,0},{16,24},{24,16},{1,9},{9,1},{17,25},{25,17},{2,10},{10... | collective-permute-start | bytes 79880 | tf_op jit(solution)/shard_map/ppermute | solution.py:34
  111.9 8.0 %collective-permute-start.19 = (f32[52,128]{1,0:T(8,128)S(1)}, f32[52,128]{1,0:T(8,128)S(1)}, u32[]{:S(2)}, u32[]{:S(2)}) collective-permute-start(f32[52,128]{1,0:T(8,128)S(1)} %shard_map.88.r_2_), channel_id=1, source_target_pairs={{0,1},{1,0},{2,3},{3,2},{4,5},{5,4},{6,7},{7,6},{8,9},{9,8},{10,11... | collective-permute-start | bytes 79880 | tf_op jit(solution)/shard_map/ppermute | solution.py:34
  111.9 8.0 %collective-permute-start.18 = (f32[52,128]{1,0:T(8,128)S(1)}, f32[52,128]{1,0:T(8,128)S(1)}, u32[]{:S(2)}, u32[]{:S(2)}) collective-permute-start(f32[52,128]{1,0:T(8,128)S(1)} %shard_map.88.r_2_), channel_id=1, source_target_pairs={{2,4},{4,2},{3,5},{5,3},{10,12},{12,10},{11,13},{13,11},{18,20},{2... | collective-permute-start | bytes 79880 | tf_op jit(solution)/shard_map/ppermute | solution.py:34
  112.5 7.3 %collective-permute-start.17 = (f32[52,128]{1,0:T(8,128)S(1)}, f32[52,128]{1,0:T(8,128)S(1)}, u32[]{:S(2)}, u32[]{:S(2)}) collective-permute-start(f32[52,128]{1,0:T(8,128)S(1)} %shard_map.88.r_2_), channel_id=1, source_target_pairs={{0,2},{2,0},{4,6},{6,4},{1,3},{3,1},{5,7},{7,5},{8,10},{10,8},{12,... | collective-permute-start | bytes 79880 | tf_op jit(solution)/shard_map/ppermute | solution.py:34
  114.6 5.2 %collective-permute-start.16 = (f32[52,128]{1,0:T(8,128)S(1)}, f32[52,128]{1,0:T(8,128)S(1)}, u32[]{:S(2)}, u32[]{:S(2)}) collective-permute-start(f32[52,128]{1,0:T(8,128)S(1)} %shard_map.88.r_2_), channel_id=1, source_target_pairs={{8,16},{16,8},{9,17},{17,9},{10,18},{18,10},{11,19},{19,11},{12,20... | collective-permute-start | bytes 79880 | tf_op jit(solution)/shard_map/ppermute | solution.py:34
  115.3 6.6 %collective-permute-start.15 = (f32[52,128]{1,0:T(8,128)S(1)}, f32[52,128]{1,0:T(8,128)S(1)}, u32[]{:S(2)}, u32[]{:S(2)}) collective-permute-start(f32[52,128]{1,0:T(8,128)S(1)} %shard_map.88.r_2_), channel_id=1, source_target_pairs={{0,8},{8,0},{16,24},{24,16},{1,9},{9,1},{17,25},{25,17},{2,10},{10... | collective-permute-start | bytes 79880 | tf_op jit(solution)/shard_map/ppermute | solution.py:34
  135.9 8.6 %collective-permute-start.24 = (f32[52,128]{1,0:T(8,128)S(1)}, f32[52,128]{1,0:T(8,128)S(1)}, u32[]{:S(2)}, u32[]{:S(2)}) collective-permute-start(f32[52,128]{1,0:T(8,128)S(1)} %shard_map.89.r_2_), channel_id=1, source_target_pairs={{0,1},{1,0},{2,3},{3,2},{4,5},{5,4},{6,7},{7,6},{8,9},{9,8},{10,11... | collective-permute-start | bytes 79880 | tf_op jit(solution)/shard_map/ppermute | solution.py:34
  135.9 8.6 %collective-permute-start.23 = (f32[52,128]{1,0:T(8,128)S(1)}, f32[52,128]{1,0:T(8,128)S(1)}, u32[]{:S(2)}, u32[]{:S(2)}) collective-permute-start(f32[52,128]{1,0:T(8,128)S(1)} %shard_map.89.r_2_), channel_id=1, source_target_pairs={{2,4},{4,2},{3,5},{5,3},{10,12},{12,10},{11,13},{13,11},{18,20},{2... | collective-permute-start | bytes 79880 | tf_op jit(solution)/shard_map/ppermute | solution.py:34
  136.6 7.9 %collective-permute-start.22 = (f32[52,128]{1,0:T(8,128)S(1)}, f32[52,128]{1,0:T(8,128)S(1)}, u32[]{:S(2)}, u32[]{:S(2)}) collective-permute-start(f32[52,128]{1,0:T(8,128)S(1)} %shard_map.89.r_2_), channel_id=1, source_target_pairs={{0,2},{2,0},{4,6},{6,4},{1,3},{3,1},{5,7},{7,5},{8,10},{10,8},{12,... | collective-permute-start | bytes 79880 | tf_op jit(solution)/shard_map/ppermute | solution.py:34
  139.2 5.3 %collective-permute-start.21 = (f32[52,128]{1,0:T(8,128)S(1)}, f32[52,128]{1,0:T(8,128)S(1)}, u32[]{:S(2)}, u32[]{:S(2)}) collective-permute-start(f32[52,128]{1,0:T(8,128)S(1)} %shard_map.89.r_2_), channel_id=1, source_target_pairs={{8,16},{16,8},{9,17},{17,9},{10,18},{18,10},{11,19},{19,11},{12,20... | collective-permute-start | bytes 79880 | tf_op jit(solution)/shard_map/ppermute | solution.py:34
  139.8 6.7 %collective-permute-start.20 = (f32[52,128]{1,0:T(8,128)S(1)}, f32[52,128]{1,0:T(8,128)S(1)}, u32[]{:S(2)}, u32[]{:S(2)}) collective-permute-start(f32[52,128]{1,0:T(8,128)S(1)} %shard_map.89.r_2_), channel_id=1, source_target_pairs={{0,8},{8,0},{16,24},{24,16},{1,9},{9,1},{17,25},{25,17},{2,10},{10... | collective-permute-start | bytes 79880 | tf_op jit(solution)/shard_map/ppermute | solution.py:34
  160.5 56.6 %copy-start.1 = (s32[52,7]{0,1:T(8,128)S(1)}, s32[52,7]{0,1:T(8,128)}, u32[]{:S(2)}) copy-start(s32[52,7]{0,1:T(8,128)} %param.7) | copy-start | bytes 4372
  160.5 8.0 %collective-permute-start.29 = (f32[52,128]{1,0:T(8,128)S(1)}, f32[52,128]{1,0:T(8,128)S(1)}, u32[]{:S(2)}, u32[]{:S(2)}) collective-permute-start(f32[52,128]{1,0:T(8,128)S(1)} %shard_map.90.r_2_), channel_id=1, source_target_pairs={{0,1},{1,0},{2,3},{3,2},{4,5},{5,4},{6,7},{7,6},{8,9},{9,8},{10,11... | collective-permute-start | bytes 79880 | tf_op jit(solution)/shard_map/ppermute | solution.py:34
  160.5 7.9 %collective-permute-start.28 = (f32[52,128]{1,0:T(8,128)S(1)}, f32[52,128]{1,0:T(8,128)S(1)}, u32[]{:S(2)}, u32[]{:S(2)}) collective-permute-start(f32[52,128]{1,0:T(8,128)S(1)} %shard_map.90.r_2_), channel_id=1, source_target_pairs={{2,4},{4,2},{3,5},{5,3},{10,12},{12,10},{11,13},{13,11},{18,20},{2... | collective-permute-start | bytes 79880 | tf_op jit(solution)/shard_map/ppermute | solution.py:34
  161.2 7.3 %collective-permute-start.27 = (f32[52,128]{1,0:T(8,128)S(1)}, f32[52,128]{1,0:T(8,128)S(1)}, u32[]{:S(2)}, u32[]{:S(2)}) collective-permute-start(f32[52,128]{1,0:T(8,128)S(1)} %shard_map.90.r_2_), channel_id=1, source_target_pairs={{0,2},{2,0},{4,6},{6,4},{1,3},{3,1},{5,7},{7,5},{8,10},{10,8},{12,... | collective-permute-start | bytes 79880 | tf_op jit(solution)/shard_map/ppermute | solution.py:34
  163.3 5.2 %collective-permute-start.26 = (f32[52,128]{1,0:T(8,128)S(1)}, f32[52,128]{1,0:T(8,128)S(1)}, u32[]{:S(2)}, u32[]{:S(2)}) collective-permute-start(f32[52,128]{1,0:T(8,128)S(1)} %shard_map.90.r_2_), channel_id=1, source_target_pairs={{8,16},{16,8},{9,17},{17,9},{10,18},{18,10},{11,19},{19,11},{12,20... | collective-permute-start | bytes 79880 | tf_op jit(solution)/shard_map/ppermute | solution.py:34
  163.9 6.6 %collective-permute-start.25 = (f32[52,128]{1,0:T(8,128)S(1)}, f32[52,128]{1,0:T(8,128)S(1)}, u32[]{:S(2)}, u32[]{:S(2)}) collective-permute-start(f32[52,128]{1,0:T(8,128)S(1)} %shard_map.90.r_2_), channel_id=1, source_target_pairs={{0,8},{8,0},{16,24},{24,16},{1,9},{9,1},{17,25},{25,17},{2,10},{10... | collective-permute-start | bytes 79880 | tf_op jit(solution)/shard_map/ppermute | solution.py:34
  184.5 9.3 %collective-permute-start.34 = (f32[52,128]{1,0:T(8,128)S(1)}, f32[52,128]{1,0:T(8,128)S(1)}, u32[]{:S(2)}, u32[]{:S(2)}) collective-permute-start(f32[52,128]{1,0:T(8,128)S(1)} %shard_map.91.r_2_), channel_id=1, source_target_pairs={{0,1},{1,0},{2,3},{3,2},{4,5},{5,4},{6,7},{7,6},{8,9},{9,8},{10,11... | collective-permute-start | bytes 79880 | tf_op jit(solution)/shard_map/ppermute | solution.py:34
  184.5 9.3 %collective-permute-start.33 = (f32[52,128]{1,0:T(8,128)S(1)}, f32[52,128]{1,0:T(8,128)S(1)}, u32[]{:S(2)}, u32[]{:S(2)}) collective-permute-start(f32[52,128]{1,0:T(8,128)S(1)} %shard_map.91.r_2_), channel_id=1, source_target_pairs={{2,4},{4,2},{3,5},{5,3},{10,12},{12,10},{11,13},{13,11},{18,20},{2... | collective-permute-start | bytes 79880 | tf_op jit(solution)/shard_map/ppermute | solution.py:34
  185.2 8.6 %collective-permute-start.32 = (f32[52,128]{1,0:T(8,128)S(1)}, f32[52,128]{1,0:T(8,128)S(1)}, u32[]{:S(2)}, u32[]{:S(2)}) collective-permute-start(f32[52,128]{1,0:T(8,128)S(1)} %shard_map.91.r_2_), channel_id=1, source_target_pairs={{0,2},{2,0},{4,6},{6,4},{1,3},{3,1},{5,7},{7,5},{8,10},{10,8},{12,... | collective-permute-start | bytes 79880 | tf_op jit(solution)/shard_map/ppermute | solution.py:34
  187.8 6.0 %collective-permute-start.31 = (f32[52,128]{1,0:T(8,128)S(1)}, f32[52,128]{1,0:T(8,128)S(1)}, u32[]{:S(2)}, u32[]{:S(2)}) collective-permute-start(f32[52,128]{1,0:T(8,128)S(1)} %shard_map.91.r_2_), channel_id=1, source_target_pairs={{8,16},{16,8},{9,17},{17,9},{10,18},{18,10},{11,19},{19,11},{12,20... | collective-permute-start | bytes 79880 | tf_op jit(solution)/shard_map/ppermute | solution.py:34
  188.5 6.7 %collective-permute-start.30 = (f32[52,128]{1,0:T(8,128)S(1)}, f32[52,128]{1,0:T(8,128)S(1)}, u32[]{:S(2)}, u32[]{:S(2)}) collective-permute-start(f32[52,128]{1,0:T(8,128)S(1)} %shard_map.91.r_2_), channel_id=1, source_target_pairs={{0,8},{8,0},{16,24},{24,16},{1,9},{9,1},{17,25},{25,17},{2,10},{10... | collective-permute-start | bytes 79880 | tf_op jit(solution)/shard_map/ppermute | solution.py:34
  209.1 8.1 %collective-permute-start.39 = (f32[52,128]{1,0:T(8,128)S(1)}, f32[52,128]{1,0:T(8,128)S(1)}, u32[]{:S(2)}, u32[]{:S(2)}) collective-permute-start(f32[52,128]{1,0:T(8,128)S(1)} %shard_map.92.r_2_), channel_id=1, source_target_pairs={{0,1},{1,0},{2,3},{3,2},{4,5},{5,4},{6,7},{7,6},{8,9},{9,8},{10,11... | collective-permute-start | bytes 79880 | tf_op jit(solution)/shard_map/ppermute | solution.py:34
  209.2 8.1 %collective-permute-start.38 = (f32[52,128]{1,0:T(8,128)S(1)}, f32[52,128]{1,0:T(8,128)S(1)}, u32[]{:S(2)}, u32[]{:S(2)}) collective-permute-start(f32[52,128]{1,0:T(8,128)S(1)} %shard_map.92.r_2_), channel_id=1, source_target_pairs={{2,4},{4,2},{3,5},{5,3},{10,12},{12,10},{11,13},{13,11},{18,20},{2... | collective-permute-start | bytes 79880 | tf_op jit(solution)/shard_map/ppermute | solution.py:34
  209.8 7.4 %collective-permute-start.37 = (f32[52,128]{1,0:T(8,128)S(1)}, f32[52,128]{1,0:T(8,128)S(1)}, u32[]{:S(2)}, u32[]{:S(2)}) collective-permute-start(f32[52,128]{1,0:T(8,128)S(1)} %shard_map.92.r_2_), channel_id=1, source_target_pairs={{0,2},{2,0},{4,6},{6,4},{1,3},{3,1},{5,7},{7,5},{8,10},{10,8},{12,... | collective-permute-start | bytes 79880 | tf_op jit(solution)/shard_map/ppermute | solution.py:34
  211.9 5.3 %collective-permute-start.36 = (f32[52,128]{1,0:T(8,128)S(1)}, f32[52,128]{1,0:T(8,128)S(1)}, u32[]{:S(2)}, u32[]{:S(2)}) collective-permute-start(f32[52,128]{1,0:T(8,128)S(1)} %shard_map.92.r_2_), channel_id=1, source_target_pairs={{8,16},{16,8},{9,17},{17,9},{10,18},{18,10},{11,19},{19,11},{12,20... | collective-permute-start | bytes 79880 | tf_op jit(solution)/shard_map/ppermute | solution.py:34
  212.6 6.6 %collective-permute-start.35 = (f32[52,128]{1,0:T(8,128)S(1)}, f32[52,128]{1,0:T(8,128)S(1)}, u32[]{:S(2)}, u32[]{:S(2)}) collective-permute-start(f32[52,128]{1,0:T(8,128)S(1)} %shard_map.92.r_2_), channel_id=1, source_target_pairs={{0,8},{8,0},{16,24},{24,16},{1,9},{9,1},{17,25},{25,17},{2,10},{10... | collective-permute-start | bytes 79880 | tf_op jit(solution)/shard_map/ppermute | solution.py:34
  233.4 1.2 collective-permute-start.40
  234.6 3.6 %collective-permute-start.43 = (f32[1,34]{1,0:T(1,128)S(1)}, f32[1,34]{1,0:T(1,128)S(1)}, u32[]{:S(2)}, u32[]{:S(2)}) collective-permute-start(f32[1,34]{1,0:T(1,128)S(1)} %fusion.2), channel_id=1, source_target_pairs={{0,6},{2,0},{4,2},{6,4},{1,7},{3,1},{5,3},{7,5},{8,14},{10,8},{12,... | collective-permute-start | bytes 416 | tf_op jit(solution)/shard_map/ppermute | solution.py:48
  236.8 4.5 %collective-permute-start.42 = (f32[1,34]{1,0:T(1,128)S(1)}, f32[1,34]{1,0:T(1,128)S(1)}, u32[]{:S(2)}, u32[]{:S(2)}) collective-permute-start(f32[1,34]{1,0:T(1,128)S(1)} %fusion.2), channel_id=1, source_target_pairs={{0,4},{2,6},{4,0},{6,2},{1,5},{3,7},{5,1},{7,3},{8,12},{10,14},{12... | collective-permute-start | bytes 416 | tf_op jit(solution)/shard_map/ppermute | solution.py:48
  236.9 5.4 %collective-permute-start.41 = (f32[1,34]{1,0:T(1,128)S(1)}, f32[1,34]{1,0:T(1,128)S(1)}, u32[]{:S(2)}, u32[]{:S(2)}) collective-permute-start(f32[1,34]{1,0:T(1,128)S(1)} %fusion.2), channel_id=1, source_target_pairs={{0,2},{2,4},{4,6},{6,0},{1,3},{3,5},{5,7},{7,1},{8,10},{10,12},{12... | collective-permute-start | bytes 416 | tf_op jit(solution)/shard_map/ppermute | solution.py:48
  242.2 3.8 %collective-permute-start.46 = (f32[1,34]{1,0:T(1,128)S(1)}, f32[1,34]{1,0:T(1,128)S(1)}, u32[]{:S(2)}, u32[]{:S(2)}) collective-permute-start(f32[1,34]{1,0:T(1,128)S(1)} %add_add_fusion.1), channel_id=1, source_target_pairs={{0,24},{8,0},{16,8},{24,16},{1,25},{9,1},{17,9},{25,17},{2,26},{10... | collective-permute-start | bytes 416 | tf_op jit(solution)/shard_map/ppermute | solution.py:48
  243.7 3.6 %collective-permute-start.45 = (f32[1,34]{1,0:T(1,128)S(1)}, f32[1,34]{1,0:T(1,128)S(1)}, u32[]{:S(2)}, u32[]{:S(2)}) collective-permute-start(f32[1,34]{1,0:T(1,128)S(1)} %add_add_fusion.1), channel_id=1, source_target_pairs={{0,16},{8,24},{16,0},{24,8},{1,17},{9,25},{17,1},{25,9},{2,18},{10... | collective-permute-start | bytes 416 | tf_op jit(solution)/shard_map/ppermute | solution.py:48
  245.5 4.5 %collective-permute-start.44 = (f32[1,34]{1,0:T(1,128)S(1)}, f32[1,34]{1,0:T(1,128)S(1)}, u32[]{:S(2)}, u32[]{:S(2)}) collective-permute-start(f32[1,34]{1,0:T(1,128)S(1)} %add_add_fusion.1), channel_id=1, source_target_pairs={{0,8},{8,16},{16,24},{24,0},{1,9},{9,17},{17,25},{25,1},{2,10},{10... | collective-permute-start | bytes 416 | tf_op jit(solution)/shard_map/ppermute | solution.py:48
  (1 other events, 7.9 us)

commit v2 on v1

--- a/solution.py
+++ b/solution.py
@@ -27,7 +27,6 @@
     received, slots, used = [], [], 0
     for axis in AXES:
         mine = lax.axis_index(axis)
-        base = used
         place = []
         for pairs in matchings(lax.axis_size(axis)):
             if pairs:
@@ -64,41 +63,49 @@
     )
 
 
-def load_kernel(a_hbm, a_ref, sem):
-    copy = pltpu.make_async_copy(a_hbm, a_ref, sem)
-    copy.start()
-    copy.wait()
-
-
-def first_kernel(faces, index_ref, a_ref, *refs):
+def group_of(count):
+    return next(g for g in (4, 3, 2, 1) if count % g == 0)
+
+
+def first_kernel(faces, index_ref, a_hbm, *refs):
     own_ref, face_refs = refs[0], refs[1 : 1 + faces]
-    prod_ref, z_ref, diag_ref, table = refs[1 + faces :]
+    prod_ref, z_ref, diag_ref, a_ref, table, sems = refs[-6:]
     nb, nk, size, _ = a_ref.shape
+    group = group_of(nb)
+
+    def piece(g):
+        part = pl.ds(g * group, group)
+        return pltpu.make_async_copy(a_hbm.at[part], a_ref.at[part], sems.at[g])
+
+    for g in range(nb // group):
+        piece(g).start()
     table[0:nb] = own_ref[...]
     for d in range(faces):
         table[(d + 1) * nb : (d + 2) * nb] = face_refs[d][...]
     sub = lax.broadcasted_iota(jnp.int32, (8, size), 0)
-
-    def body(b, _):
-        total = jnp.zeros((8, size), jnp.float32)
-        for k in range(nk):
-            block = a_ref[b, k]
-            if k == 0:
-                eye = lax.broadcasted_iota(jnp.int32, (size, size), 0) == (
-                    lax.broadcasted_iota(jnp.int32, (size, size), 1)
-                )
-                diag = jnp.sum(jnp.where(eye, block, 0.0), axis=0, keepdims=True)
-                diag_ref[pl.ds(b, 1), :] = diag
-            rows = table[index_ref[b * nk + k]]
-            rows_high, rows_low = split(rows)
-            high, low = split(block)
-            product = dot_t(rows_high, high) + (dot_t(rows_low, high) + dot_t(rows_high, low))
-            total = total + product
-            prod_ref[b * nk + k] = jnp.where(sub == 7, rows, product)
-        z_ref[pl.ds(b, 1), :] = total[0:1, :] / diag
+    eye = lax.broadcasted_iota(jnp.int32, (size, size), 0) == (
+        lax.broadcasted_iota(jnp.int32, (size, size), 1)
+    )
+
+    def body(g, _):
+        piece(g).wait()
+        for u in range(group):
+            b = g * group + u
+            diag = jnp.sum(jnp.where(eye, a_ref[b, 0], 0.0), axis=0, keepdims=True)
+            diag_ref[pl.ds(b, 1), :] = diag
+            total = jnp.zeros((8, size), jnp.float32)
+            for k in range(nk):
+                rows = table[index_ref[b * nk + k]]
+                rows_high, rows_low = split(rows)
+                high, low = split(a_ref[b, k])
+                both = dot_t(jnp.concatenate([rows_high, rows_low], axis=0), high)
+                product = both[0:8] + (both[8:16] + dot_t(rows_high, low))
+                total = total + product
+                prod_ref[b * nk + k] = jnp.where(sub == 7, rows, product)
+            z_ref[pl.ds(b, 1), :] = total[0:1, :] / diag
         return 0
 
-    lax.fori_loop(0, nb, body, 0)
+    lax.fori_loop(0, nb // group, body, 0)
 
 
 def step_kernel(faces, last, index_ref, a_ref, *refs):
@@ -111,19 +118,22 @@
     table[0:nb, :] = own_ref[...]
     for d in range(faces):
         table[(d + 1) * stride : (d + 1) * stride + nb, :] = face_refs[d][...]
-    ones = jnp.ones((8, size), jnp.bfloat16)
-
-    def body(b, _):
-        acc = None
-        for k in range(nk):
-            term = a_ref[b, k] * table[pl.ds(index_ref[b * nk + k], 1), :]
-            acc = term if acc is None else acc + term
-        high, low = split(acc)
-        row = dot_t(ones, high) + dot_t(ones, low)
-        z_ref[pl.ds(b, 1), :] = row[0:1, :] / diag_ref[pl.ds(b, 1), :]
-        return 0
-
-    lax.fori_loop(0, nb, body, 0, unroll=2 if nb % 2 == 0 else 1)
+    width = -(-nb // size) * size
+    lane = lax.broadcasted_iota(jnp.int32, (size, width), 1)
+    group = group_of(nb)
+
+    def body(g, columns):
+        for u in range(group):
+            b = g * group + u
+            acc = None
+            for k in range(nk):
+                term = a_ref[b, k] * table[pl.ds(index_ref[b * nk + k], 1), :]
+                acc = term if acc is None else acc + term
+            columns = jnp.where(lane == b, jnp.sum(acc, axis=1, keepdims=True), columns)
+        return columns
+
+    columns = lax.fori_loop(0, nb // group, body, jnp.zeros((size, width), jnp.float32))
+    z_ref[...] = columns.T[0:nb, :] / diag_ref[...]
     if last:
         before, now = own_ref[...], z_ref[...]
         outs[1][0:1, :] = jnp.sum(before * before, axis=0, keepdims=True)
@@ -165,7 +175,7 @@
         c_ref[start : start + n, :] = ns * base.astype(jnp.int32)
 
 
-def call(kernel, out_shape, in_specs, scratch=(), limit=34 * MIB):
+def call(kernel, out_shape, in_specs, scratch=(), limit=8 * MIB):
     many = isinstance(out_shape, (tuple, list))
     return pl.pallas_call(
         kernel,
@@ -188,13 +198,6 @@
         me = me * lax.axis_size(axis) + lax.axis_index(axis)
     strides = (lax.axis_size("gy") * lax.axis_size("gz"), lax.axis_size("gz"), 1)
     ids = jnp.stack([me] + [me + sign * s for s in strides for sign in (-1, 1)])
-
-    a_here = call(
-        load_kernel,
-        pltpu.VMEM(a_blocks.shape, f32),
-        [ANY],
-        [pltpu.SemaphoreType.DMA],
-    )(a_blocks)
 
     names = jnp.broadcast_to(agg_ids.astype(f32)[:, None, None], (nb, 1, size))
     x_own = jnp.concatenate([start_vec[:, None, :], p0_blocks, names], axis=1)
@@ -209,16 +212,24 @@
     first_index = (slot * nb + row).reshape(-1)
     index = (slot * stride + row).reshape(-1)
 
-    prod, current, diag = call(
+    mark = jnp.where(jnp.arange(devices) == me, agg_counts[0].astype(f32), 0.0)
+    x_flat = x_own.reshape(nb * 8, size)
+    early = (index, ids, block_cols, mark, x_flat)
+
+    prod, current, diag, a_here = call(
         lambda *r: first_kernel(faces, *r),
         (
             jax.ShapeDtypeStruct((nb * nk, 8, size), f32),
             jax.ShapeDtypeStruct((nb, size), f32),
             jax.ShapeDtypeStruct((nb, size), f32),
+            pltpu.VMEM(a_blocks.shape, f32),
         ),
-        [SMEM, VMEM, VMEM] + [VMEM] * faces,
-        [pltpu.VMEM(((faces + 1) * nb, 8, size), f32)],
-    )(first_index, a_here, x_own, *x_faces)
+        [SMEM, ANY, VMEM] + [VMEM] * faces + [ANY] * len(early),
+        [
+            pltpu.VMEM(((faces + 1) * nb, 8, size), f32),
+            pltpu.SemaphoreType.DMA((nb // group_of(nb),)),
+        ],
+    )(first_index, a_blocks, x_own, *x_faces, *early)
 
     for turn in range(1, ITERS):
         last = turn == ITERS - 1
@@ -234,7 +245,6 @@
         )(index, a_here, current, *received, diag)
         current = results[0]
 
-    mark = jnp.where(jnp.arange(devices) == me, agg_counts[0].astype(f32), 0.0)
     totals = summed(jnp.concatenate([jnp.sum(results[1], axis=1), mark])[None, :])
 
     smoothed, p_cols, power_vec = call(
@@ -250,7 +260,7 @@
         totals,
         block_cols,
         prod.reshape(nb * nk * 8, size),
-        x_own.reshape(nb * 8, size),
+        x_flat,
         diag,
         current,
     )

time: 254 us -> 154 us (0.61)
  Pallas kernels: 141 us -> 40.7 us
  waiting for transfers between devices: 22.9 us -> 30.8 us
  local copies, waits for them, and re-layouts: 11 us -> 3.85 us
    pallas_call x7, Pallas kernels: 98 us -> 22.6 us  [local(): call(lambda *r, last=last: step_kernel(faces, last, *r), tuple(shapes), [...]
    pallas_call x1, Pallas kernels: 33.4 us -> 16.2 us  [local(): call(lambda *r: first_kernel(faces, *r), (jax.ShapeDtypeStruct((nb * nk,...]
    ppermute x40, waiting for transfers between devices: 13.3 us -> 21.1 us  [exchange(): received.append(lax.ppermute(value, axis, pairs))]
    pallas_call x1 -> x0, Pallas kernels: 7.8 us -> none  [local(): call(load_kernel, pltpu.VMEM(a_blocks.shape, f32), [ANY], [pltpu.Semaphor...]
    unnamed x7 -> x3, local copies, waits for them, and re-layouts: 9.6 us -> 2.42 us
  transfers between devices with their start and end apart: 47 -> 47, of which waited for: 13 -> 14; matrix products, arithmetic and copies ran while one was open for 1% -> 1% of each run, Pallas kernels for 3% -> 0%
where the time goes in v2:
time: 154 us; the launch traced here: 153 us
  starting transfers between devices  74.2 us (48%)
  Pallas kernels  40.7 us (26%)
  waiting for transfers between devices  30.8 us (20%)
  local copies, waits for them, and re-layouts  3.85 us (2%)
  other arithmetic  1.8 us (1%)
  between operations  1.7 us (1%)
    ppermute x40, starting transfers between devices, exchange(): received.append(lax.ppermute(value, axis, pairs))  67.5 us
    pallas_call x7, Pallas kernels, local(): call(lambda *r, last=last: step_kernel(faces, last, *r), tuple(shapes), [...  22.6 us
    ppermute x40, waiting for transfers between devices, exchange(): received.append(lax.ppermute(value, axis, pairs))  21.1 us
    pallas_call x1, Pallas kernels, local(): call(lambda *r: first_kernel(faces, *r), (jax.ShapeDtypeStruct((nb * nk,...  16.2 us
    ppermute x7, waiting for transfers between devices, summed(): lax.ppermute(value, axis, [(i, (i + step) % count) for i in range(count)])  9.77 us
    ppermute x7, starting transfers between devices, summed(): lax.ppermute(value, axis, [(i, (i + step) % count) for i in range(count)])  6.69 us
  transfers between devices with their start and end apart: 47, of which 14 were waited for; matrix products, arithmetic and copies ran while one was open for 1% of the time, Pallas kernels for 0%

profile of v2, /device:TPU:0, one launch (start us, length us, event | category | flops | bytes accessed | tf_op | source)
XLA Modules:
  0.0 153.1 jit_solution(13561965944515089801)
XLA Ops:
  1.3 0.8 broadcast_in_dim.43
  2.1 1.0 copy.15
  4.5 5.5 %collective-permute-start.2 = (f32[52,8,128]{2,1,0:T(8,128)S(1)}, f32[52,8,128]{2,1,0:T(8,128)S(1)}, u32[]{:S(2)}, u32[]{:S(2)}) collective-permute-start(f32[52,8,128]{2,1,0:T(8,128)S(1)} %pad_maximum_fusion.r_2_), channel_id=1, source_target_pairs={{0,2},{2,0},{4,6},{6,4},{1,3},{3,1},{5,7},{7,5},{8,10},{10,8},{12,... | collective-permute-start | bytes 638984 | tf_op jit(solution)/shard_map/ppermute | solution.py:33
  10.6 4.3 %collective-permute-start = (f32[52,8,128]{2,1,0:T(8,128)S(1)}, f32[52,8,128]{2,1,0:T(8,128)S(1)}, u32[]{:S(2)}, u32[]{:S(2)}) collective-permute-start(f32[52,8,128]{2,1,0:T(8,128)S(1)} %pad_maximum_fusion.r_2_), channel_id=1, source_target_pairs={{0,8},{8,0},{16,24},{24,16},{1,9},{9,1},{17,25},{25,17},{2,10},{10... | collective-permute-start | bytes 638984 | tf_op jit(solution)/shard_map/ppermute | solution.py:33
  15.5 0.8 copy.16.r_10_.r_2_
  16.3 0.7 multiply_add_fusion
  17.7 6.7 %collective-permute-done.r_3_ = f32[52,8,128]{2,1,0:T(8,128)S(1)} collective-permute-done((f32[52,8,128]{2,1,0:T(8,128)S(1)}, f32[52,8,128]{2,1,0:T(8,128)S(1)}, u32[]{:S(2)}, u32[]{:S(2)}) %collective-permute-start) | collective-permute-done | bytes 213024 | tf_op jit(solution)/shard_map/ppermute | solution.py:33
  24.4 16.2 %shard_map.85 = (f32[364,8,128]{2,1,0:T(8,128)S(1)}, f32[52,128]{1,0:T(8,128)S(1)}, f32[52,128]{1,0:T(8,128)S(1)}, f32[52,7,128,128]{3,2,1,0:T(8,128)S(1)}) custom-call(s32[364]{0:T(512)S(1)} %reshape.23.r_0_, f32[52,7,128,128]{3,2,1,0:T(8,128)} %r_1_.1, f32[52,8,128]{2,1,0:T(8,128)S(1)} %pad_maximum_fusion.r_2_, ...), custom_call_target="tpu_custom_call" | custom-call | tf_op jit(solution)/shard_map/pallas_call | solution.py:219
  40.7 0.7 collective-permute-start.8
  41.3 2.1 %collective-permute-start.7 = (f32[52,128]{1,0:T(8,128)S(1)}, f32[52,128]{1,0:T(8,128)S(1)}, u32[]{:S(2)}, u32[]{:S(2)}) collective-permute-start(f32[52,128]{1,0:T(8,128)S(1)} %get-tuple-element.13.r_2_), channel_id=1, source_target_pairs={{0,2},{2,0},{4,6},{6,4},{1,3},{3,1},{5,7},{7,5},{8,10},{10,8},{12,... | collective-permute-start | bytes 79880 | tf_op jit(solution)/shard_map/ppermute | solution.py:33
  44.1 2.3 %collective-permute-start.5 = (f32[52,128]{1,0:T(8,128)S(1)}, f32[52,128]{1,0:T(8,128)S(1)}, u32[]{:S(2)}, u32[]{:S(2)}) collective-permute-start(f32[52,128]{1,0:T(8,128)S(1)} %get-tuple-element.13.r_2_), channel_id=1, source_target_pairs={{0,8},{8,0},{16,24},{24,16},{1,9},{9,1},{17,25},{25,17},{2,10},{10... | collective-permute-start | bytes 79880 | tf_op jit(solution)/shard_map/ppermute | solution.py:33
  46.4 2.0 %collective-permute-done.5.r_3_ = f32[52,128]{1,0:T(8,128)S(1)} collective-permute-done((f32[52,128]{1,0:T(8,128)S(1)}, f32[52,128]{1,0:T(8,128)S(1)}, u32[]{:S(2)}, u32[]{:S(2)}) %collective-permute-start.5) | collective-permute-done | bytes 26656 | tf_op jit(solution)/shard_map/ppermute | solution.py:33
  48.4 3.2 %shard_map.86.r_2_ = f32[52,128]{1,0:T(8,128)S(1)} custom-call(s32[364]{0:T(512)S(1)} %reshape.22.r_8_.r_0_, f32[52,7,128,128]{3,2,1,0:T(8,128)S(1)} %get-tuple-element.12.r_1_, f32[52,128]{1,0:T(8,128)S(1)} %get-tuple-element.13.r_2_, f32[52,128]{1,0:T(8,128)S(1)} %collective-permute-done.5.r_3_, f32[52,128]{1,0:T(8,128)S(1)} %collective-permute-done.6.r_4_, ...), custom_call_target="tpu_custom_call" | custom-call | tf_op jit(solution)/shard_map/pallas_call | solution.py:240
  52.4 2.9 %collective-permute-start.12 = (f32[52,128]{1,0:T(8,128)S(1)}, f32[52,128]{1,0:T(8,128)S(1)}, u32[]{:S(2)}, u32[]{:S(2)}) collective-permute-start(f32[52,128]{1,0:T(8,128)S(1)} %shard_map.86.r_2_), channel_id=1, source_target_pairs={{0,2},{2,0},{4,6},{6,4},{1,3},{3,1},{5,7},{7,5},{8,10},{10,8},{12,... | collective-permute-start | bytes 79880 | tf_op jit(solution)/shard_map/ppermute | solution.py:33
  56.0 4.6 %collective-permute-start.10 = (f32[52,128]{1,0:T(8,128)S(1)}, f32[52,128]{1,0:T(8,128)S(1)}, u32[]{:S(2)}, u32[]{:S(2)}) collective-permute-start(f32[52,128]{1,0:T(8,128)S(1)} %shard_map.86.r_2_), channel_id=1, source_target_pairs={{0,8},{8,0},{16,24},{24,16},{1,9},{9,1},{17,25},{25,17},{2,10},{10... | collective-permute-start | bytes 79880 | tf_op jit(solution)/shard_map/ppermute | solution.py:33
  60.6 2.0 %collective-permute-done.10.r_3_ = f32[52,128]{1,0:T(8,128)S(1)} collective-permute-done((f32[52,128]{1,0:T(8,128)S(1)}, f32[52,128]{1,0:T(8,128)S(1)}, u32[]{:S(2)}, u32[]{:S(2)}) %collective-permute-start.10) | collective-permute-done | bytes 26656 | tf_op jit(solution)/shard_map/ppermute | solution.py:33
  62.6 3.2 %shard_map.87.r_2_ = f32[52,128]{1,0:T(8,128)S(1)} custom-call(s32[364]{0:T(512)S(1)} %reshape.22.r_8_.r_0_, f32[52,7,128,128]{3,2,1,0:T(8,128)S(1)} %get-tuple-element.12.r_1_, f32[52,128]{1,0:T(8,128)S(1)} %shard_map.86.r_2_, f32[52,128]{1,0:T(8,128)S(1)} %collective-permute-done.10.r_3_, f32[52,128]{1,0:T(8,128)S(1)} %collective-permute-done.11.r_4_, ...), custom_call_target="tpu_custom_call" | custom-call | tf_op jit(solution)/shard_map/pallas_call | solution.py:240
  66.6 2.1 %collective-permute-start.17 = (f32[52,128]{1,0:T(8,128)S(1)}, f32[52,128]{1,0:T(8,128)S(1)}, u32[]{:S(2)}, u32[]{:S(2)}) collective-permute-start(f32[52,128]{1,0:T(8,128)S(1)} %shard_map.87.r_2_), channel_id=1, source_target_pairs={{0,2},{2,0},{4,6},{6,4},{1,3},{3,1},{5,7},{7,5},{8,10},{10,8},{12,... | collective-permute-start | bytes 79880 | tf_op jit(solution)/shard_map/ppermute | solution.py:33
  69.3 4.5 %collective-permute-start.15 = (f32[52,128]{1,0:T(8,128)S(1)}, f32[52,128]{1,0:T(8,128)S(1)}, u32[]{:S(2)}, u32[]{:S(2)}) collective-permute-start(f32[52,128]{1,0:T(8,128)S(1)} %shard_map.87.r_2_), channel_id=1, source_target_pairs={{0,8},{8,0},{16,24},{24,16},{1,9},{9,1},{17,25},{25,17},{2,10},{10... | collective-permute-start | bytes 79880 | tf_op jit(solution)/shard_map/ppermute | solution.py:33
  73.9 2.0 %collective-permute-done.15.r_3_ = f32[52,128]{1,0:T(8,128)S(1)} collective-permute-done((f32[52,128]{1,0:T(8,128)S(1)}, f32[52,128]{1,0:T(8,128)S(1)}, u32[]{:S(2)}, u32[]{:S(2)}) %collective-permute-start.15) | collective-permute-done | bytes 26656 | tf_op jit(solution)/shard_map/ppermute | solution.py:33
  76.0 3.2 %shard_map.88.r_2_ = f32[52,128]{1,0:T(8,128)S(1)} custom-call(s32[364]{0:T(512)S(1)} %reshape.22.r_8_.r_0_, f32[52,7,128,128]{3,2,1,0:T(8,128)S(1)} %get-tuple-element.12.r_1_, f32[52,128]{1,0:T(8,128)S(1)} %shard_map.87.r_2_, f32[52,128]{1,0:T(8,128)S(1)} %collective-permute-done.15.r_3_, f32[52,128]{1,0:T(8,128)S(1)} %collective-permute-done.16.r_4_, ...), custom_call_target="tpu_custom_call" | custom-call | tf_op jit(solution)/shard_map/pallas_call | solution.py:240
  79.9 2.6 %collective-permute-start.22 = (f32[52,128]{1,0:T(8,128)S(1)}, f32[52,128]{1,0:T(8,128)S(1)}, u32[]{:S(2)}, u32[]{:S(2)}) collective-permute-start(f32[52,128]{1,0:T(8,128)S(1)} %shard_map.88.r_2_), channel_id=1, source_target_pairs={{0,2},{2,0},{4,6},{6,4},{1,3},{3,1},{5,7},{7,5},{8,10},{10,8},{12,... | collective-permute-start | bytes 79880 | tf_op jit(solution)/shard_map/ppermute | solution.py:33
  83.2 4.6 %collective-permute-start.20 = (f32[52,128]{1,0:T(8,128)S(1)}, f32[52,128]{1,0:T(8,128)S(1)}, u32[]{:S(2)}, u32[]{:S(2)}) collective-permute-start(f32[52,128]{1,0:T(8,128)S(1)} %shard_map.88.r_2_), channel_id=1, source_target_pairs={{0,8},{8,0},{16,24},{24,16},{1,9},{9,1},{17,25},{25,17},{2,10},{10... | collective-permute-start | bytes 79880 | tf_op jit(solution)/shard_map/ppermute | solution.py:33
  87.9 2.0 %collective-permute-done.20.r_3_ = f32[52,128]{1,0:T(8,128)S(1)} collective-permute-done((f32[52,128]{1,0:T(8,128)S(1)}, f32[52,128]{1,0:T(8,128)S(1)}, u32[]{:S(2)}, u32[]{:S(2)}) %collective-permute-start.20) | collective-permute-done | bytes 26656 | tf_op jit(solution)/shard_map/ppermute | solution.py:33
  89.9 3.2 %shard_map.89.r_2_ = f32[52,128]{1,0:T(8,128)S(1)} custom-call(s32[364]{0:T(512)S(1)} %reshape.22.r_8_.r_0_, f32[52,7,128,128]{3,2,1,0:T(8,128)S(1)} %get-tuple-element.12.r_1_, f32[52,128]{1,0:T(8,128)S(1)} %shard_map.88.r_2_, f32[52,128]{1,0:T(8,128)S(1)} %collective-permute-done.20.r_3_, f32[52,128]{1,0:T(8,128)S(1)} %collective-permute-done.21.r_4_, ...), custom_call_target="tpu_custom_call" | custom-call | tf_op jit(solution)/shard_map/pallas_call | solution.py:240
  93.9 2.1 %collective-permute-start.27 = (f32[52,128]{1,0:T(8,128)S(1)}, f32[52,128]{1,0:T(8,128)S(1)}, u32[]{:S(2)}, u32[]{:S(2)}) collective-permute-start(f32[52,128]{1,0:T(8,128)S(1)} %shard_map.89.r_2_), channel_id=1, source_target_pairs={{0,2},{2,0},{4,6},{6,4},{1,3},{3,1},{5,7},{7,5},{8,10},{10,8},{12,... | collective-permute-start | bytes 79880 | tf_op jit(solution)/shard_map/ppermute | solution.py:33
  96.6 4.5 %collective-permute-start.25 = (f32[52,128]{1,0:T(8,128)S(1)}, f32[52,128]{1,0:T(8,128)S(1)}, u32[]{:S(2)}, u32[]{:S(2)}) collective-permute-start(f32[52,128]{1,0:T(8,128)S(1)} %shard_map.89.r_2_), channel_id=1, source_target_pairs={{0,8},{8,0},{16,24},{24,16},{1,9},{9,1},{17,25},{25,17},{2,10},{10... | collective-permute-start | bytes 79880 | tf_op jit(solution)/shard_map/ppermute | solution.py:33
  101.2 2.0 %collective-permute-done.25.r_3_ = f32[52,128]{1,0:T(8,128)S(1)} collective-permute-done((f32[52,128]{1,0:T(8,128)S(1)}, f32[52,128]{1,0:T(8,128)S(1)}, u32[]{:S(2)}, u32[]{:S(2)}) %collective-permute-start.25) | collective-permute-done | bytes 26656 | tf_op jit(solution)/shard_map/ppermute | solution.py:33
  103.2 3.2 %shard_map.90.r_2_ = f32[52,128]{1,0:T(8,128)S(1)} custom-call(s32[364]{0:T(512)S(1)} %reshape.22.r_8_.r_0_, f32[52,7,128,128]{3,2,1,0:T(8,128)S(1)} %get-tuple-element.12.r_1_, f32[52,128]{1,0:T(8,128)S(1)} %shard_map.89.r_2_, f32[52,128]{1,0:T(8,128)S(1)} %collective-permute-done.25.r_3_, f32[52,128]{1,0:T(8,128)S(1)} %collective-permute-done.26.r_4_, ...), custom_call_target="tpu_custom_call" | custom-call | tf_op jit(solution)/shard_map/pallas_call | solution.py:240
  107.2 2.6 %collective-permute-start.32 = (f32[52,128]{1,0:T(8,128)S(1)}, f32[52,128]{1,0:T(8,128)S(1)}, u32[]{:S(2)}, u32[]{:S(2)}) collective-permute-start(f32[52,128]{1,0:T(8,128)S(1)} %shard_map.90.r_2_), channel_id=1, source_target_pairs={{0,2},{2,0},{4,6},{6,4},{1,3},{3,1},{5,7},{7,5},{8,10},{10,8},{12,... | collective-permute-start | bytes 79880 | tf_op jit(solution)/shard_map/ppermute | solution.py:33
  110.5 4.6 %collective-permute-start.30 = (f32[52,128]{1,0:T(8,128)S(1)}, f32[52,128]{1,0:T(8,128)S(1)}, u32[]{:S(2)}, u32[]{:S(2)}) collective-permute-start(f32[52,128]{1,0:T(8,128)S(1)} %shard_map.90.r_2_), channel_id=1, source_target_pairs={{0,8},{8,0},{16,24},{24,16},{1,9},{9,1},{17,25},{25,17},{2,10},{10... | collective-permute-start | bytes 79880 | tf_op jit(solution)/shard_map/ppermute | solution.py:33
  115.1 2.0 %collective-permute-done.30.r_3_ = f32[52,128]{1,0:T(8,128)S(1)} collective-permute-done((f32[52,128]{1,0:T(8,128)S(1)}, f32[52,128]{1,0:T(8,128)S(1)}, u32[]{:S(2)}, u32[]{:S(2)}) %collective-permute-start.30) | collective-permute-done | bytes 26656 | tf_op jit(solution)/shard_map/ppermute | solution.py:33
  117.2 3.2 %shard_map.91.r_2_ = f32[52,128]{1,0:T(8,128)S(1)} custom-call(s32[364]{0:T(512)S(1)} %reshape.22.r_8_.r_0_, f32[52,7,128,128]{3,2,1,0:T(8,128)S(1)} %get-tuple-element.12.r_1_, f32[52,128]{1,0:T(8,128)S(1)} %shard_map.90.r_2_, f32[52,128]{1,0:T(8,128)S(1)} %collective-permute-done.30.r_3_, f32[52,128]{1,0:T(8,128)S(1)} %collective-permute-done.31.r_4_, ...), custom_call_target="tpu_custom_call" | custom-call | tf_op jit(solution)/shard_map/pallas_call | solution.py:240
  121.1 2.1 %collective-permute-start.37 = (f32[52,128]{1,0:T(8,128)S(1)}, f32[52,128]{1,0:T(8,128)S(1)}, u32[]{:S(2)}, u32[]{:S(2)}) collective-permute-start(f32[52,128]{1,0:T(8,128)S(1)} %shard_map.91.r_2_), channel_id=1, source_target_pairs={{0,2},{2,0},{4,6},{6,4},{1,3},{3,1},{5,7},{7,5},{8,10},{10,8},{12,... | collective-permute-start | bytes 79880 | tf_op jit(solution)/shard_map/ppermute | solution.py:33
  123.9 4.5 %collective-permute-start.35 = (f32[52,128]{1,0:T(8,128)S(1)}, f32[52,128]{1,0:T(8,128)S(1)}, u32[]{:S(2)}, u32[]{:S(2)}) collective-permute-start(f32[52,128]{1,0:T(8,128)S(1)} %shard_map.91.r_2_), channel_id=1, source_target_pairs={{0,8},{8,0},{16,24},{24,16},{1,9},{9,1},{17,25},{25,17},{2,10},{10... | collective-permute-start | bytes 79880 | tf_op jit(solution)/shard_map/ppermute | solution.py:33
  128.4 2.0 %collective-permute-done.35.r_3_ = f32[52,128]{1,0:T(8,128)S(1)} collective-permute-done((f32[52,128]{1,0:T(8,128)S(1)}, f32[52,128]{1,0:T(8,128)S(1)}, u32[]{:S(2)}, u32[]{:S(2)}) %collective-permute-start.35) | collective-permute-done | bytes 26656 | tf_op jit(solution)/shard_map/ppermute | solution.py:33
  130.5 3.2 %shard_map.92 = (f32[52,128]{1,0:T(8,128)S(1)}, f32[2,128]{1,0:T(2,128)S(1)}) custom-call(s32[364]{0:T(512)S(1)} %reshape.22.r_8_.r_0_, f32[52,7,128,128]{3,2,1,0:T(8,128)S(1)} %get-tuple-element.12.r_1_, f32[52,128]{1,0:T(8,128)S(1)} %shard_map.91.r_2_, f32[52,128]{1,0:T(8,128)S(1)} %collective-permute-done.35.r_3_, ...), custom_call_target="tpu_custom_call" | custom-call | tf_op jit(solution)/shard_map/pallas_call | solution.py:240
  133.9 1.2 collective-permute-done.40
  135.2 2.2 %collective-permute-start.43 = (f32[1,34]{1,0:T(1,128)S(1)}, f32[1,34]{1,0:T(1,128)S(1)}, u32[]{:S(2)}, u32[]{:S(2)}) collective-permute-start(f32[1,34]{1,0:T(1,128)S(1)} %fusion.1), channel_id=1, source_target_pairs={{0,6},{2,0},{4,2},{6,4},{1,7},{3,1},{5,3},{7,5},{8,14},{10,8},{12,... | collective-permute-start | bytes 416 | tf_op jit(solution)/shard_map/ppermute | solution.py:47
  138.0 0.7 collective-permute-done.43
  138.7 3.1 %collective-permute-done.42 = f32[1,34]{1,0:T(1,128)S(1)} collective-permute-done((f32[1,34]{1,0:T(1,128)S(1)}, f32[1,34]{1,0:T(1,128)S(1)}, u32[]{:S(2)}, u32[]{:S(2)}) %collective-permute-start.42) | collective-permute-done | bytes 168 | tf_op jit(solution)/shard_map/ppermute | solution.py:47
  141.8 0.9 collective-permute-done.41
  142.7 1.5 collective-permute-start.46
  144.2 1.8 %collective-permute-start.45 = (f32[1,34]{1,0:T(1,128)S(1)}, f32[1,34]{1,0:T(1,128)S(1)}, u32[]{:S(2)}, u32[]{:S(2)}) collective-permute-start(f32[1,34]{1,0:T(1,128)S(1)} %add_add_fusion.1), channel_id=1, source_target_pairs={{0,16},{8,24},{16,0},{24,8},{1,17},{9,25},{17,1},{25,9},{2,18},{10... | collective-permute-start | bytes 416 | tf_op jit(solution)/shard_map/ppermute | solution.py:47
  146.6 1.2 collective-permute-done.45
  147.8 2.7 %collective-permute-done.44 = f32[1,34]{1,0:T(1,128)S(1)} collective-permute-done((f32[1,34]{1,0:T(1,128)S(1)}, f32[1,34]{1,0:T(1,128)S(1)}, u32[]{:S(2)}, u32[]{:S(2)}) %collective-permute-start.44) | collective-permute-done | bytes 168 | tf_op jit(solution)/shard_map/ppermute | solution.py:47
  150.5 2.0 %shard_map.93 = (f32[7,6,52,128]{3,2,1,0:T(8,128)}, s32[52,7]{1,0:T(8,128)S(1)}, f32[52,128]{1,0:T(8,128)}) custom-call(s32[7]{0:T(128)S(1)} %stack.31.r_9_.r_0_, f32[1,34]{1,0:T(1,128)S(1)} %add_add_fusion.r_1_, s32[52,7]{1,0:T(8,128)S(1)} %copy.16.r_10_.r_2_, f32[2912,128]{1,0:T(8,128)S(1)} %bitcast.16, f32[416,128]{1,0:T(8,128)S(1)} %fusion.2.r_12_.r_4_, ...), custom_call_target="tpu_custom_call" | custom-call | tf_op jit(solution)/shard_map/pallas_call | solution.py:250
  152.5 0.7 copy.18
  (75 shorter events, 14.0 us)
Async XLA Ops:
  3.2 14.4 %collective-permute-start.4 = (f32[52,8,128]{2,1,0:T(8,128)S(1)}, f32[52,8,128]{2,1,0:T(8,128)S(1)}, u32[]{:S(2)}, u32[]{:S(2)}) collective-permute-start(f32[52,8,128]{2,1,0:T(8,128)S(1)} %pad_maximum_fusion.r_2_), channel_id=1, source_target_pairs={{0,1},{1,0},{2,3},{3,2},{4,5},{5,4},{6,7},{7,6},{8,9},{9,8},{10,11... | collective-permute-start | bytes 638984 | tf_op jit(solution)/shard_map/ppermute | solution.py:33
  3.8 13.9 %collective-permute-start.3 = (f32[52,8,128]{2,1,0:T(8,128)S(1)}, f32[52,8,128]{2,1,0:T(8,128)S(1)}, u32[]{:S(2)}, u32[]{:S(2)}) collective-permute-start(f32[52,8,128]{2,1,0:T(8,128)S(1)} %pad_maximum_fusion.r_2_), channel_id=1, source_target_pairs={{2,4},{4,2},{3,5},{5,3},{10,12},{12,10},{11,13},{13,11},{18,20},{2... | collective-permute-start | bytes 638984 | tf_op jit(solution)/shard_map/ppermute | solution.py:33
  4.5 13.2 %collective-permute-start.2 = (f32[52,8,128]{2,1,0:T(8,128)S(1)}, f32[52,8,128]{2,1,0:T(8,128)S(1)}, u32[]{:S(2)}, u32[]{:S(2)}) collective-permute-start(f32[52,8,128]{2,1,0:T(8,128)S(1)} %pad_maximum_fusion.r_2_), channel_id=1, source_target_pairs={{0,2},{2,0},{4,6},{6,4},{1,3},{3,1},{5,7},{7,5},{8,10},{10,8},{12,... | collective-permute-start | bytes 638984 | tf_op jit(solution)/shard_map/ppermute | solution.py:33
  9.9 7.8 %collective-permute-start.1 = (f32[52,8,128]{2,1,0:T(8,128)S(1)}, f32[52,8,128]{2,1,0:T(8,128)S(1)}, u32[]{:S(2)}, u32[]{:S(2)}) collective-permute-start(f32[52,8,128]{2,1,0:T(8,128)S(1)} %pad_maximum_fusion.r_2_), channel_id=1, source_target_pairs={{8,16},{16,8},{9,17},{17,9},{10,18},{18,10},{11,19},{19,11},{12,20... | collective-permute-start | bytes 638984 | tf_op jit(solution)/shard_map/ppermute | solution.py:33
  10.6 13.8 %collective-permute-start = (f32[52,8,128]{2,1,0:T(8,128)S(1)}, f32[52,8,128]{2,1,0:T(8,128)S(1)}, u32[]{:S(2)}, u32[]{:S(2)}) collective-permute-start(f32[52,8,128]{2,1,0:T(8,128)S(1)} %pad_maximum_fusion.r_2_), channel_id=1, source_target_pairs={{0,8},{8,0},{16,24},{24,16},{1,9},{9,1},{17,25},{25,17},{2,10},{10... | collective-permute-start | bytes 638984 | tf_op jit(solution)/shard_map/ppermute | solution.py:33
  40.6 5.8 %collective-permute-start.9 = (f32[52,128]{1,0:T(8,128)S(1)}, f32[52,128]{1,0:T(8,128)S(1)}, u32[]{:S(2)}, u32[]{:S(2)}) collective-permute-start(f32[52,128]{1,0:T(8,128)S(1)} %get-tuple-element.13.r_2_), channel_id=1, source_target_pairs={{0,1},{1,0},{2,3},{3,2},{4,5},{5,4},{6,7},{7,6},{8,9},{9,8},{10,11... | collective-permute-start | bytes 79880 | tf_op jit(solution)/shard_map/ppermute | solution.py:33
  40.7 5.7 %collective-permute-start.8 = (f32[52,128]{1,0:T(8,128)S(1)}, f32[52,128]{1,0:T(8,128)S(1)}, u32[]{:S(2)}, u32[]{:S(2)}) collective-permute-start(f32[52,128]{1,0:T(8,128)S(1)} %get-tuple-element.13.r_2_), channel_id=1, source_target_pairs={{2,4},{4,2},{3,5},{5,3},{10,12},{12,10},{11,13},{13,11},{18,20},{2... | collective-permute-start | bytes 79880 | tf_op jit(solution)/shard_map/ppermute | solution.py:33
  41.3 5.0 %collective-permute-start.7 = (f32[52,128]{1,0:T(8,128)S(1)}, f32[52,128]{1,0:T(8,128)S(1)}, u32[]{:S(2)}, u32[]{:S(2)}) collective-permute-start(f32[52,128]{1,0:T(8,128)S(1)} %get-tuple-element.13.r_2_), channel_id=1, source_target_pairs={{0,2},{2,0},{4,6},{6,4},{1,3},{3,1},{5,7},{7,5},{8,10},{10,8},{12,... | collective-permute-start | bytes 79880 | tf_op jit(solution)/shard_map/ppermute | solution.py:33
  43.4 3.0 %collective-permute-start.6 = (f32[52,128]{1,0:T(8,128)S(1)}, f32[52,128]{1,0:T(8,128)S(1)}, u32[]{:S(2)}, u32[]{:S(2)}) collective-permute-start(f32[52,128]{1,0:T(8,128)S(1)} %get-tuple-element.13.r_2_), channel_id=1, source_target_pairs={{8,16},{16,8},{9,17},{17,9},{10,18},{18,10},{11,19},{19,11},{12,20... | collective-permute-start | bytes 79880 | tf_op jit(solution)/shard_map/ppermute | solution.py:33
  44.1 4.4 %collective-permute-start.5 = (f32[52,128]{1,0:T(8,128)S(1)}, f32[52,128]{1,0:T(8,128)S(1)}, u32[]{:S(2)}, u32[]{:S(2)}) collective-permute-start(f32[52,128]{1,0:T(8,128)S(1)} %get-tuple-element.13.r_2_), channel_id=1, source_target_pairs={{0,8},{8,0},{16,24},{24,16},{1,9},{9,1},{17,25},{25,17},{2,10},{10... | collective-permute-start | bytes 79880 | tf_op jit(solution)/shard_map/ppermute | solution.py:33
  51.6 8.9 %collective-permute-start.14 = (f32[52,128]{1,0:T(8,128)S(1)}, f32[52,128]{1,0:T(8,128)S(1)}, u32[]{:S(2)}, u32[]{:S(2)}) collective-permute-start(f32[52,128]{1,0:T(8,128)S(1)} %shard_map.86.r_2_), channel_id=1, source_target_pairs={{0,1},{1,0},{2,3},{3,2},{4,5},{5,4},{6,7},{7,6},{8,9},{9,8},{10,11... | collective-permute-start | bytes 79880 | tf_op jit(solution)/shard_map/ppermute | solution.py:33
  51.7 8.9 %collective-permute-start.13 = (f32[52,128]{1,0:T(8,128)S(1)}, f32[52,128]{1,0:T(8,128)S(1)}, u32[]{:S(2)}, u32[]{:S(2)}) collective-permute-start(f32[52,128]{1,0:T(8,128)S(1)} %shard_map.86.r_2_), channel_id=1, source_target_pairs={{2,4},{4,2},{3,5},{5,3},{10,12},{12,10},{11,13},{13,11},{18,20},{2... | collective-permute-start | bytes 79880 | tf_op jit(solution)/shard_map/ppermute | solution.py:33
  52.4 8.2 %collective-permute-start.12 = (f32[52,128]{1,0:T(8,128)S(1)}, f32[52,128]{1,0:T(8,128)S(1)}, u32[]{:S(2)}, u32[]{:S(2)}) collective-permute-start(f32[52,128]{1,0:T(8,128)S(1)} %shard_map.86.r_2_), channel_id=1, source_target_pairs={{0,2},{2,0},{4,6},{6,4},{1,3},{3,1},{5,7},{7,5},{8,10},{10,8},{12,... | collective-permute-start | bytes 79880 | tf_op jit(solution)/shard_map/ppermute | solution.py:33
  55.3 5.3 %collective-permute-start.11 = (f32[52,128]{1,0:T(8,128)S(1)}, f32[52,128]{1,0:T(8,128)S(1)}, u32[]{:S(2)}, u32[]{:S(2)}) collective-permute-start(f32[52,128]{1,0:T(8,128)S(1)} %shard_map.86.r_2_), channel_id=1, source_target_pairs={{8,16},{16,8},{9,17},{17,9},{10,18},{18,10},{11,19},{19,11},{12,20... | collective-permute-start | bytes 79880 | tf_op jit(solution)/shard_map/ppermute | solution.py:33
  56.0 6.7 %collective-permute-start.10 = (f32[52,128]{1,0:T(8,128)S(1)}, f32[52,128]{1,0:T(8,128)S(1)}, u32[]{:S(2)}, u32[]{:S(2)}) collective-permute-start(f32[52,128]{1,0:T(8,128)S(1)} %shard_map.86.r_2_), channel_id=1, source_target_pairs={{0,8},{8,0},{16,24},{24,16},{1,9},{9,1},{17,25},{25,17},{2,10},{10... | collective-permute-start | bytes 79880 | tf_op jit(solution)/shard_map/ppermute | solution.py:33
  65.9 8.0 %collective-permute-start.19 = (f32[52,128]{1,0:T(8,128)S(1)}, f32[52,128]{1,0:T(8,128)S(1)}, u32[]{:S(2)}, u32[]{:S(2)}) collective-permute-start(f32[52,128]{1,0:T(8,128)S(1)} %shard_map.87.r_2_), channel_id=1, source_target_pairs={{0,1},{1,0},{2,3},{3,2},{4,5},{5,4},{6,7},{7,6},{8,9},{9,8},{10,11... | collective-permute-start | bytes 79880 | tf_op jit(solution)/shard_map/ppermute | solution.py:33
  65.9 8.0 %collective-permute-start.18 = (f32[52,128]{1,0:T(8,128)S(1)}, f32[52,128]{1,0:T(8,128)S(1)}, u32[]{:S(2)}, u32[]{:S(2)}) collective-permute-start(f32[52,128]{1,0:T(8,128)S(1)} %shard_map.87.r_2_), channel_id=1, source_target_pairs={{2,4},{4,2},{3,5},{5,3},{10,12},{12,10},{11,13},{13,11},{18,20},{2... | collective-permute-start | bytes 79880 | tf_op jit(solution)/shard_map/ppermute | solution.py:33
  66.6 7.3 %collective-permute-start.17 = (f32[52,128]{1,0:T(8,128)S(1)}, f32[52,128]{1,0:T(8,128)S(1)}, u32[]{:S(2)}, u32[]{:S(2)}) collective-permute-start(f32[52,128]{1,0:T(8,128)S(1)} %shard_map.87.r_2_), channel_id=1, source_target_pairs={{0,2},{2,0},{4,6},{6,4},{1,3},{3,1},{5,7},{7,5},{8,10},{10,8},{12,... | collective-permute-start | bytes 79880 | tf_op jit(solution)/shard_map/ppermute | solution.py:33
  68.7 5.2 %collective-permute-start.16 = (f32[52,128]{1,0:T(8,128)S(1)}, f32[52,128]{1,0:T(8,128)S(1)}, u32[]{:S(2)}, u32[]{:S(2)}) collective-permute-start(f32[52,128]{1,0:T(8,128)S(1)} %shard_map.87.r_2_), channel_id=1, source_target_pairs={{8,16},{16,8},{9,17},{17,9},{10,18},{18,10},{11,19},{19,11},{12,20... | collective-permute-start | bytes 79880 | tf_op jit(solution)/shard_map/ppermute | solution.py:33
  69.3 6.6 %collective-permute-start.15 = (f32[52,128]{1,0:T(8,128)S(1)}, f32[52,128]{1,0:T(8,128)S(1)}, u32[]{:S(2)}, u32[]{:S(2)}) collective-permute-start(f32[52,128]{1,0:T(8,128)S(1)} %shard_map.87.r_2_), channel_id=1, source_target_pairs={{0,8},{8,0},{16,24},{24,16},{1,9},{9,1},{17,25},{25,17},{2,10},{10... | collective-permute-start | bytes 79880 | tf_op jit(solution)/shard_map/ppermute | solution.py:33
  79.2 8.7 %collective-permute-start.24 = (f32[52,128]{1,0:T(8,128)S(1)}, f32[52,128]{1,0:T(8,128)S(1)}, u32[]{:S(2)}, u32[]{:S(2)}) collective-permute-start(f32[52,128]{1,0:T(8,128)S(1)} %shard_map.88.r_2_), channel_id=1, source_target_pairs={{0,1},{1,0},{2,3},{3,2},{4,5},{5,4},{6,7},{7,6},{8,9},{9,8},{10,11... | collective-permute-start | bytes 79880 | tf_op jit(solution)/shard_map/ppermute | solution.py:33
  79.3 8.6 %collective-permute-start.23 = (f32[52,128]{1,0:T(8,128)S(1)}, f32[52,128]{1,0:T(8,128)S(1)}, u32[]{:S(2)}, u32[]{:S(2)}) collective-permute-start(f32[52,128]{1,0:T(8,128)S(1)} %shard_map.88.r_2_), channel_id=1, source_target_pairs={{2,4},{4,2},{3,5},{5,3},{10,12},{12,10},{11,13},{13,11},{18,20},{2... | collective-permute-start | bytes 79880 | tf_op jit(solution)/shard_map/ppermute | solution.py:33
  79.9 7.9 %collective-permute-start.22 = (f32[52,128]{1,0:T(8,128)S(1)}, f32[52,128]{1,0:T(8,128)S(1)}, u32[]{:S(2)}, u32[]{:S(2)}) collective-permute-start(f32[52,128]{1,0:T(8,128)S(1)} %shard_map.88.r_2_), channel_id=1, source_target_pairs={{0,2},{2,0},{4,6},{6,4},{1,3},{3,1},{5,7},{7,5},{8,10},{10,8},{12,... | collective-permute-start | bytes 79880 | tf_op jit(solution)/shard_map/ppermute | solution.py:33
  82.6 5.3 %collective-permute-start.21 = (f32[52,128]{1,0:T(8,128)S(1)}, f32[52,128]{1,0:T(8,128)S(1)}, u32[]{:S(2)}, u32[]{:S(2)}) collective-permute-start(f32[52,128]{1,0:T(8,128)S(1)} %shard_map.88.r_2_), channel_id=1, source_target_pairs={{8,16},{16,8},{9,17},{17,9},{10,18},{18,10},{11,19},{19,11},{12,20... | collective-permute-start | bytes 79880 | tf_op jit(solution)/shard_map/ppermute | solution.py:33
  83.2 6.7 %collective-permute-start.20 = (f32[52,128]{1,0:T(8,128)S(1)}, f32[52,128]{1,0:T(8,128)S(1)}, u32[]{:S(2)}, u32[]{:S(2)}) collective-permute-start(f32[52,128]{1,0:T(8,128)S(1)} %shard_map.88.r_2_), channel_id=1, source_target_pairs={{0,8},{8,0},{16,24},{24,16},{1,9},{9,1},{17,25},{25,17},{2,10},{10... | collective-permute-start | bytes 79880 | tf_op jit(solution)/shard_map/ppermute | solution.py:33
  93.1 8.0 %collective-permute-start.29 = (f32[52,128]{1,0:T(8,128)S(1)}, f32[52,128]{1,0:T(8,128)S(1)}, u32[]{:S(2)}, u32[]{:S(2)}) collective-permute-start(f32[52,128]{1,0:T(8,128)S(1)} %shard_map.89.r_2_), channel_id=1, source_target_pairs={{0,1},{1,0},{2,3},{3,2},{4,5},{5,4},{6,7},{7,6},{8,9},{9,8},{10,11... | collective-permute-start | bytes 79880 | tf_op jit(solution)/shard_map/ppermute | solution.py:33
  93.2 8.0 %collective-permute-start.28 = (f32[52,128]{1,0:T(8,128)S(1)}, f32[52,128]{1,0:T(8,128)S(1)}, u32[]{:S(2)}, u32[]{:S(2)}) collective-permute-start(f32[52,128]{1,0:T(8,128)S(1)} %shard_map.89.r_2_), channel_id=1, source_target_pairs={{2,4},{4,2},{3,5},{5,3},{10,12},{12,10},{11,13},{13,11},{18,20},{2... | collective-permute-start | bytes 79880 | tf_op jit(solution)/shard_map/ppermute | solution.py:33
  93.9 7.3 %collective-permute-start.27 = (f32[52,128]{1,0:T(8,128)S(1)}, f32[52,128]{1,0:T(8,128)S(1)}, u32[]{:S(2)}, u32[]{:S(2)}) collective-permute-start(f32[52,128]{1,0:T(8,128)S(1)} %shard_map.89.r_2_), channel_id=1, source_target_pairs={{0,2},{2,0},{4,6},{6,4},{1,3},{3,1},{5,7},{7,5},{8,10},{10,8},{12,... | collective-permute-start | bytes 79880 | tf_op jit(solution)/shard_map/ppermute | solution.py:33
  95.9 5.2 %collective-permute-start.26 = (f32[52,128]{1,0:T(8,128)S(1)}, f32[52,128]{1,0:T(8,128)S(1)}, u32[]{:S(2)}, u32[]{:S(2)}) collective-permute-start(f32[52,128]{1,0:T(8,128)S(1)} %shard_map.89.r_2_), channel_id=1, source_target_pairs={{8,16},{16,8},{9,17},{17,9},{10,18},{18,10},{11,19},{19,11},{12,20... | collective-permute-start | bytes 79880 | tf_op jit(solution)/shard_map/ppermute | solution.py:33
  96.6 6.6 %collective-permute-start.25 = (f32[52,128]{1,0:T(8,128)S(1)}, f32[52,128]{1,0:T(8,128)S(1)}, u32[]{:S(2)}, u32[]{:S(2)}) collective-permute-start(f32[52,128]{1,0:T(8,128)S(1)} %shard_map.89.r_2_), channel_id=1, source_target_pairs={{0,8},{8,0},{16,24},{24,16},{1,9},{9,1},{17,25},{25,17},{2,10},{10... | collective-permute-start | bytes 79880 | tf_op jit(solution)/shard_map/ppermute | solution.py:33
  106.4 8.7 %collective-permute-start.34 = (f32[52,128]{1,0:T(8,128)S(1)}, f32[52,128]{1,0:T(8,128)S(1)}, u32[]{:S(2)}, u32[]{:S(2)}) collective-permute-start(f32[52,128]{1,0:T(8,128)S(1)} %shard_map.90.r_2_), channel_id=1, source_target_pairs={{0,1},{1,0},{2,3},{3,2},{4,5},{5,4},{6,7},{7,6},{8,9},{9,8},{10,11... | collective-permute-start | bytes 79880 | tf_op jit(solution)/shard_map/ppermute | solution.py:33
  106.5 8.6 %collective-permute-start.33 = (f32[52,128]{1,0:T(8,128)S(1)}, f32[52,128]{1,0:T(8,128)S(1)}, u32[]{:S(2)}, u32[]{:S(2)}) collective-permute-start(f32[52,128]{1,0:T(8,128)S(1)} %shard_map.90.r_2_), channel_id=1, source_target_pairs={{2,4},{4,2},{3,5},{5,3},{10,12},{12,10},{11,13},{13,11},{18,20},{2... | collective-permute-start | bytes 79880 | tf_op jit(solution)/shard_map/ppermute | solution.py:33
  107.2 7.9 %collective-permute-start.32 = (f32[52,128]{1,0:T(8,128)S(1)}, f32[52,128]{1,0:T(8,128)S(1)}, u32[]{:S(2)}, u32[]{:S(2)}) collective-permute-start(f32[52,128]{1,0:T(8,128)S(1)} %shard_map.90.r_2_), channel_id=1, source_target_pairs={{0,2},{2,0},{4,6},{6,4},{1,3},{3,1},{5,7},{7,5},{8,10},{10,8},{12,... | collective-permute-start | bytes 79880 | tf_op jit(solution)/shard_map/ppermute | solution.py:33
  109.8 5.3 %collective-permute-start.31 = (f32[52,128]{1,0:T(8,128)S(1)}, f32[52,128]{1,0:T(8,128)S(1)}, u32[]{:S(2)}, u32[]{:S(2)}) collective-permute-start(f32[52,128]{1,0:T(8,128)S(1)} %shard_map.90.r_2_), channel_id=1, source_target_pairs={{8,16},{16,8},{9,17},{17,9},{10,18},{18,10},{11,19},{19,11},{12,20... | collective-permute-start | bytes 79880 | tf_op jit(solution)/shard_map/ppermute | solution.py:33
  110.5 6.7 %collective-permute-start.30 = (f32[52,128]{1,0:T(8,128)S(1)}, f32[52,128]{1,0:T(8,128)S(1)}, u32[]{:S(2)}, u32[]{:S(2)}) collective-permute-start(f32[52,128]{1,0:T(8,128)S(1)} %shard_map.90.r_2_), channel_id=1, source_target_pairs={{0,8},{8,0},{16,24},{24,16},{1,9},{9,1},{17,25},{25,17},{2,10},{10... | collective-permute-start | bytes 79880 | tf_op jit(solution)/shard_map/ppermute | solution.py:33
  120.4 8.0 %collective-permute-start.39 = (f32[52,128]{1,0:T(8,128)S(1)}, f32[52,128]{1,0:T(8,128)S(1)}, u32[]{:S(2)}, u32[]{:S(2)}) collective-permute-start(f32[52,128]{1,0:T(8,128)S(1)} %shard_map.91.r_2_), channel_id=1, source_target_pairs={{0,1},{1,0},{2,3},{3,2},{4,5},{5,4},{6,7},{7,6},{8,9},{9,8},{10,11... | collective-permute-start | bytes 79880 | tf_op jit(solution)/shard_map/ppermute | solution.py:33
  120.5 8.0 %collective-permute-start.38 = (f32[52,128]{1,0:T(8,128)S(1)}, f32[52,128]{1,0:T(8,128)S(1)}, u32[]{:S(2)}, u32[]{:S(2)}) collective-permute-start(f32[52,128]{1,0:T(8,128)S(1)} %shard_map.91.r_2_), channel_id=1, source_target_pairs={{2,4},{4,2},{3,5},{5,3},{10,12},{12,10},{11,13},{13,11},{18,20},{2... | collective-permute-start | bytes 79880 | tf_op jit(solution)/shard_map/ppermute | solution.py:33
  121.1 7.3 %collective-permute-start.37 = (f32[52,128]{1,0:T(8,128)S(1)}, f32[52,128]{1,0:T(8,128)S(1)}, u32[]{:S(2)}, u32[]{:S(2)}) collective-permute-start(f32[52,128]{1,0:T(8,128)S(1)} %shard_map.91.r_2_), channel_id=1, source_target_pairs={{0,2},{2,0},{4,6},{6,4},{1,3},{3,1},{5,7},{7,5},{8,10},{10,8},{12,... | collective-permute-start | bytes 79880 | tf_op jit(solution)/shard_map/ppermute | solution.py:33
  123.2 5.2 %collective-permute-start.36 = (f32[52,128]{1,0:T(8,128)S(1)}, f32[52,128]{1,0:T(8,128)S(1)}, u32[]{:S(2)}, u32[]{:S(2)}) collective-permute-start(f32[52,128]{1,0:T(8,128)S(1)} %shard_map.91.r_2_), channel_id=1, source_target_pairs={{8,16},{16,8},{9,17},{17,9},{10,18},{18,10},{11,19},{19,11},{12,20... | collective-permute-start | bytes 79880 | tf_op jit(solution)/shard_map/ppermute | solution.py:33
  123.9 6.6 %collective-permute-start.35 = (f32[52,128]{1,0:T(8,128)S(1)}, f32[52,128]{1,0:T(8,128)S(1)}, u32[]{:S(2)}, u32[]{:S(2)}) collective-permute-start(f32[52,128]{1,0:T(8,128)S(1)} %shard_map.91.r_2_), channel_id=1, source_target_pairs={{0,8},{8,0},{16,24},{24,16},{1,9},{9,1},{17,25},{25,17},{2,10},{10... | collective-permute-start | bytes 79880 | tf_op jit(solution)/shard_map/ppermute | solution.py:33
  133.9 1.2 collective-permute-start.40
  135.2 3.6 %collective-permute-start.43 = (f32[1,34]{1,0:T(1,128)S(1)}, f32[1,34]{1,0:T(1,128)S(1)}, u32[]{:S(2)}, u32[]{:S(2)}) collective-permute-start(f32[1,34]{1,0:T(1,128)S(1)} %fusion.1), channel_id=1, source_target_pairs={{0,6},{2,0},{4,2},{6,4},{1,7},{3,1},{5,3},{7,5},{8,14},{10,8},{12,... | collective-permute-start | bytes 416 | tf_op jit(solution)/shard_map/ppermute | solution.py:47
  137.4 4.5 %collective-permute-start.42 = (f32[1,34]{1,0:T(1,128)S(1)}, f32[1,34]{1,0:T(1,128)S(1)}, u32[]{:S(2)}, u32[]{:S(2)}) collective-permute-start(f32[1,34]{1,0:T(1,128)S(1)} %fusion.1), channel_id=1, source_target_pairs={{0,4},{2,6},{4,0},{6,2},{1,5},{3,7},{5,1},{7,3},{8,12},{10,14},{12... | collective-permute-start | bytes 416 | tf_op jit(solution)/shard_map/ppermute | solution.py:47
  137.4 5.4 %collective-permute-start.41 = (f32[1,34]{1,0:T(1,128)S(1)}, f32[1,34]{1,0:T(1,128)S(1)}, u32[]{:S(2)}, u32[]{:S(2)}) collective-permute-start(f32[1,34]{1,0:T(1,128)S(1)} %fusion.1), channel_id=1, source_target_pairs={{0,2},{2,4},{4,6},{6,0},{1,3},{3,5},{5,7},{7,1},{8,10},{10,12},{12... | collective-permute-start | bytes 416 | tf_op jit(solution)/shard_map/ppermute | solution.py:47
  142.7 3.9 %collective-permute-start.46 = (f32[1,34]{1,0:T(1,128)S(1)}, f32[1,34]{1,0:T(1,128)S(1)}, u32[]{:S(2)}, u32[]{:S(2)}) collective-permute-start(f32[1,34]{1,0:T(1,128)S(1)} %add_add_fusion.1), channel_id=1, source_target_pairs={{0,24},{8,0},{16,8},{24,16},{1,25},{9,1},{17,9},{25,17},{2,26},{10... | collective-permute-start | bytes 416 | tf_op jit(solution)/shard_map/ppermute | solution.py:47
  144.2 3.6 %collective-permute-start.45 = (f32[1,34]{1,0:T(1,128)S(1)}, f32[1,34]{1,0:T(1,128)S(1)}, u32[]{:S(2)}, u32[]{:S(2)}) collective-permute-start(f32[1,34]{1,0:T(1,128)S(1)} %add_add_fusion.1), channel_id=1, source_target_pairs={{0,16},{8,24},{16,0},{24,8},{1,17},{9,25},{17,1},{25,9},{2,18},{10... | collective-permute-start | bytes 416 | tf_op jit(solution)/shard_map/ppermute | solution.py:47
  146.0 4.5 %collective-permute-start.44 = (f32[1,34]{1,0:T(1,128)S(1)}, f32[1,34]{1,0:T(1,128)S(1)}, u32[]{:S(2)}, u32[]{:S(2)}) collective-permute-start(f32[1,34]{1,0:T(1,128)S(1)} %add_add_fusion.1), channel_id=1, source_target_pairs={{0,8},{8,16},{16,24},{24,0},{1,9},{9,17},{17,25},{25,1},{2,10},{10... | collective-permute-start | bytes 416 | tf_op jit(solution)/shard_map/ppermute | solution.py:47
